TPU v7x, 256 devices: a whole 4x4x8 slice. The times are simulated.
256 devices in a mesh: seq: 64 (over z, y, core), head: 4 (over x).
Axes of the slice: x: 4, y: 4, z: 8, core: 2. Of those that a mesh axis runs over, the one named last changes fastest.
Arguments:
- query_rows: bfloat16 [32768, 4096], P('seq', 'head'), may hold values from -6 to 6
- key_rows: bfloat16 [32768, 4096], P('seq', 'head'), may hold values from -2 to 2
- value_rows: bfloat16 [32768, 4096], P('seq', 'head'), may hold values from -6 to 6
- key_gain: float32 [32], P('head'), may hold values from 0.9 to 1.85, as said below
- regularizer: float32 [32], P('head'), may hold values from 0.5 to 4
Outputs:
- readout: bfloat16 [32768, 4096], P('seq', 'head')
Inputs may be any that keep to these rules, and one draw needn't show every extreme that they name: `key_gain`: one positive gain for each head.
All inputs are finite; a program needn't handle non-finite values.
Results may differ from a plain program's by a relative error of at most 0.006.
Values sent between devices are 32-bit elements; how exact they have to be, the bound alone decides.
No kernel may reach another device: no remote copies, remote signals or barrier semaphores. Data moves between devices by JAX's collectives and lax.ppermute only.
A program may use at most 192 MiB of HBM per device.

v0:
```python
import jax
import jax.numpy as jnp
from jax import lax
from jax.sharding import Mesh
from jax.sharding import PartitionSpec as P

DH = 128
NS_STEPS = 8
REFINE = 2
SEQ = ("seq_0", "seq_1", "seq_2")


highest = lax.Precision.HIGHEST


def filled_with(value, identity):
    return jnp.zeros_like(value) + jnp.asarray(identity, value.dtype)


def prefix_by_axis(value, axes, combine, identity):
    before = start = filled_with(value, identity)
    subtotal = value
    for axis in reversed(axes):
        length, place = (lax.axis_size(axis), lax.axis_index(axis))
        pieces = lax.all_gather(subtotal, axis)
        inside, subtotal = (start, start)
        for k in range(length):
            passed = k < place
            subtotal = combine(subtotal, pieces[k])
            inside = jnp.where(passed, subtotal, inside)
        before = combine(inside, before)
    return before


def contract_rows(left, right):
    return lax.dot_general(
        left, right, (((1,), (1,)), ((), ())), preferred_element_type=jnp.float32
    )


def add_states(earlier, later):
    return earlier + later


def invert_scaled(end_matrix, spectral_bound):
    identity = jnp.eye(end_matrix.shape[-1], dtype=jnp.float32)
    approx = identity[None, :, :] / spectral_bound[:, None, None]
    for iteration in range(NS_STEPS):
        product = jnp.einsum("hij,hjk->hik", end_matrix, approx, precision=highest)
        approx = jnp.einsum("hij,hjk->hik", approx, 2.0 * identity - product, precision=highest)
    return approx


def solve_head(operands):
    query_head, key_head, value_head, base_matrix, precond, cross_matrix = operands
    length = query_head.shape[0]
    causal = jnp.arange(length)[:, None] >= jnp.arange(length)[None, :]
    query_float = query_head.astype(jnp.float32)
    solution = jnp.dot(query_float, precond, precision=highest)
    for repeat in range(REFINE):
        scores = jnp.where(
            causal, contract_rows(solution.astype(jnp.bfloat16), key_head), 0.0
        ).astype(jnp.bfloat16)
        in_block = jnp.dot(scores, key_head, preferred_element_type=jnp.float32)
        residual = query_float - jnp.dot(solution, base_matrix, precision=highest) - in_block
        solution = solution + jnp.dot(residual, precond, precision=highest)
    scores = jnp.where(causal, contract_rows(solution.astype(jnp.bfloat16), key_head), 0.0).astype(
        jnp.bfloat16
    )
    total = jnp.dot(solution, cross_matrix, precision=highest) + jnp.dot(
        scores, value_head, preferred_element_type=jnp.float32
    )
    return total.astype(jnp.bfloat16)


def body(query_rows, key_rows, value_rows, key_gain, regularizer):
    row_count = query_rows.shape[0]
    head_count = key_gain.shape[0]
    query_split = query_rows.reshape(row_count, head_count, DH)
    key_split = key_rows.reshape(row_count, head_count, DH)
    value_split = value_rows.reshape(row_count, head_count, DH)
    scaled = (key_split.astype(jnp.float32) * key_gain[None, :, None]).astype(jnp.bfloat16)
    gram_block = jnp.einsum("thd,the->hde", scaled, scaled, preferred_element_type=jnp.float32)
    cross_block = jnp.einsum(
        "thd,the->hde", scaled, value_split, preferred_element_type=jnp.float32
    )
    payload = jnp.stack([gram_block, cross_block])
    earlier = prefix_by_axis(payload, SEQ, add_states, jnp.zeros_like(payload))
    earlier_gram = earlier[0]
    earlier_cross = earlier[1]
    identity = jnp.eye(DH, dtype=jnp.float32)
    base_matrix = regularizer[:, None, None] * identity + earlier_gram
    end_matrix = base_matrix + gram_block
    spectral_bound = jnp.sqrt(jnp.sum(end_matrix * end_matrix, axis=(1, 2)))
    precond = invert_scaled(end_matrix, spectral_bound)
    readout = lax.map(
        solve_head,
        (
            jnp.transpose(query_split, (1, 0, 2)),
            jnp.transpose(scaled, (1, 0, 2)),
            jnp.transpose(value_split, (1, 0, 2)),
            base_matrix,
            precond,
            earlier_cross,
        ),
    )
    return jnp.transpose(readout, (1, 0, 2)).reshape(row_count, head_count * DH)


def solution(mesh):
    torus = Mesh(
        mesh.devices.reshape(8, 4, 2, mesh.shape["head"]), ("seq_0", "seq_1", "seq_2", "head")
    )
    in_specs = (P(SEQ, "head"), P(SEQ, "head"), P(SEQ, "head"), P("head"), P("head"))
    out_specs = P(SEQ, "head")
    return jax.shard_map(body, mesh=torus, in_specs=in_specs, out_specs=out_specs, check_vma=False)
```

profile of v0, /device:TPU:1, one launch (start us, length us, event | category | flops | bytes accessed | tf_op | source)
XLA Modules:
  0.0 289.9 jit_solution(16953520821809289704)
XLA Ops:
  6.5 1.6 copy.19
  11.2 20.5 %all-gather.8.cloned.1.call-done = f32[4,8,128,128]{3,2,1,0:T(8,128)} async-done(((f32[2,8,128,128]{3,2,1,0:T(8,128)}), f32[4,8,128,128]{3,2,1,0:T(8,128)}) %all-gather.8.cloned.1.call-update) | async-done | bytes 2097168 | tf_op jit(solution)/shard_map/all_gather | solution.py:25
  31.8 2.6 slice_add_fusion.10
  34.5 51.3 %all-gather.10.cloned.1.call-done = f32[8,8,128,128]{3,2,1,0:T(8,128)} async-done(((f32[2,8,128,128]{3,2,1,0:T(8,128)}), f32[8,8,128,128]{3,2,1,0:T(8,128)}) %all-gather.10.cloned.1.call-update) | async-done | bytes 4194320 | tf_op jit(solution)/shard_map/all_gather | solution.py:25
  85.8 3.5 %fusion.68 = f32[1,2,8,128,128]{4,3,2,1,0:T(8,128)} fusion(f32[8,8,128,128]{3,2,1,0:T(8,128)} %all-gather.10.cloned.1.call-done), kind=kLoop, calls=%fused_computation.84 | loop fusion | flops 786432 | bytes 5242880 | tf_op jit(solution)/shard_map/add | solution.py:42
  89.3 2.4 copy.18
  93.1 90.7 %all-gather.6.cloned.1.call-done = f32[8,2,8,128,128]{4,3,2,1,0:T(8,128)} async-done(((f32[1,2,8,128,128]{4,3,2,1,0:T(8,128)}), f32[8,2,8,128,128]{4,3,2,1,0:T(8,128)}) %all-gather.6.cloned.1.call-update) | async-done | bytes 8388624 | tf_op jit(solution)/shard_map/all_gather | solution.py:25
  183.8 6.4 %fusion.67 = f32[1,2,8,128,128]{4,3,2,1,0:T(8,128)S(1)} fusion(f32[8,2,8,128,128]{4,3,2,1,0:T(8,128)} %all-gather.6.cloned.1.call-done, f32[8,8,128,128]{3,2,1,0:T(8,128)} %all-gather.10.cloned.1.call-done, f32[4,8,128,128]{3,2,1,0:T(8,128)S(1)} %copy-done, pred[]{:T(512)S(6)} %gt.51, pred[]{:T(512)S(6)} %gt.52, pred[]{:T(512)S(6)} %gt.53, pred[]{:T(512)S(6)} %gt.54, ...), kind=kLoop, calls=%fused_computation.76 | loop fusion | flops 7077888 | bytes 15728654 | tf_op jit(solution)/shard_map/add | solution.py:42
  202.1 78.9 %while.10 = (s32[]{:T(128)}, bf16[8,512,128]{2,1,0:T(8,128)(2,1)}, bf16[8,512,128]{1,2,0:T(8,128)(2,1)}, f32[8,128,128]{2,1,0:T(8,128)S(1)}, f32[8,128,128]{2,1,...) while((s32[]{:T(128)}, bf16[8,512,128]{2,1,0:T(8,128)(2,1)}, ...), condition=%wide.region_2.3_spmd, body=%wide.region_1.2_spmd.sunk | while | flops 1009844224 | bytes 7738481 | solution.py:96
  204.8 1.4 fusion.176
  207.0 1.4 fusion.177
  210.0 2.1 fusion.179
  214.7 1.4 fusion.176
  216.8 1.4 fusion.177
  219.8 2.0 fusion.179
  224.5 1.4 fusion.176
  226.7 1.4 fusion.177
  229.7 2.0 fusion.179
  234.4 1.4 fusion.176
  236.5 1.4 fusion.177
  239.5 2.0 fusion.179
  244.2 1.4 fusion.176
  246.4 1.4 fusion.177
  249.4 2.0 fusion.179
  254.1 1.4 fusion.176
  259.3 2.1 fusion.179
  266.1 1.4 fusion.177
  269.1 2.0 fusion.179
  273.8 1.4 fusion.176
  276.0 1.4 fusion.177
  279.0 2.0 fusion.179
  281.0 2.4 copy_bitcast_fusion
  (113 shorter events, 58.6 us)
Async XLA Ops:
  6.5 1.6 copy-start.4
  6.5 2.2 copy-start.5
  6.5 25.2 %all-gather.8.cloned.1.call-start = ((), (), s32[]{:S(2)}) async-start(), calls=%async_computation.1 | async-start | bytes 3145728 | tf_op jit(solution)/shard_map/all_gather | solution.py:25
  8.7 1.1 copy-start.1
  9.3 0.8 copy-start.2
  11.2 74.6 %all-gather.10.cloned.1.call-start = ((), (), s32[]{:S(2)}) async-start(), calls=%async_computation.2 | async-start | bytes 5242880 | tf_op jit(solution)/shard_map/all_gather | solution.py:25
  34.4 149.4 %all-gather.6.cloned.1.call-start = ((), (), s32[]{:S(2)}) async-start(), calls=%async_computation | async-start | bytes 9437184 | tf_op jit(solution)/shard_map/all_gather | solution.py:25
  89.3 94.5 %copy-start = (f32[4,8,128,128]{3,2,1,0:T(8,128)S(1)}, f32[4,8,128,128]{3,2,1,0:T(8,128)}, u32[]{:S(2)}) copy-start(f32[4,8,128,128]{3,2,1,0:T(8,128)} %all-gather.8.cloned.1.call-done) | copy-start | bytes 6291460
  93.1 97.9 %copy-start.3 = (f32[8,128,128]{2,1,0:T(8,128)S(1)}, f32[8,128,128]{2,1,0:T(8,128)}, u32[]{:S(2)}) copy-start(f32[8,128,128]{2,1,0:T(8,128)} %copy-done.2) | copy-start | bytes 1572868
  93.1 97.9 %copy-start.6 = (f32[8]{0:T(128)S(1)}, f32[8]{0:T(128)}, u32[]{:S(2)}) copy-start(f32[8]{0:T(128)} %param.11) | copy-start | bytes 100
Sparse Core Ops, SparseCore 0:
  11.3 20.4 all-gather.7
  34.5 51.1 all-gather.9
  89.4 94.4 all-gather.5
where the time goes:
time: 291 us; the launch traced here: 290 us
  waiting for transfers between devices  163 us (56%)
  matrix products  81.8 us (28%)
  local copies, waits for them, and re-layouts  16.4 us (6%)
  other arithmetic  15.2 us (5%)
  between operations  13.4 us (5%)
    all_gather x3, waiting for transfers between devices, prefix_by_axis(): pieces = lax.all_gather(subtotal, axis)  163 us
    dot_general x16, matrix products, solve_head(): in_block = jnp.dot(scores, key_head, preferred_element_type=jnp.float32)  22.5 us
    dot_general x8, matrix products, solve_head(): jnp.dot(scores, value_head, preferred_element_type=jnp.float32)  16.4 us
    add x3, other arithmetic, add_states(): return earlier + later  12.5 us
    dot_general x8, matrix products, solve_head(): solution = jnp.dot(query_float, precond, precision=highest)  9.74 us
    dot_general x8, matrix products, solve_head(): jnp.dot(solution, cross_matrix, precision=highest)  9.65 us
    dynamic_slice x16, local copies, waits for them, and re-layouts, body(): lax.map(solve_head, (jnp.transpose(query_split, (1, 0, 2)), jnp.transpose...  8.29 us
    dot_general x16, matrix products, solve_head(): jnp.dot(solution, base_matrix, precision=highest)  5.95 us
  transfers between devices with their start and end apart: 3, of which 3 were waited for; matrix products, arithmetic and copies ran while one was open for 1% of the time, Pallas kernels for 0%

commit v1 on v0

v1 whole, which is shorter than its diff:
```python
import functools
import jax
import jax.numpy as jnp
from jax import lax
from jax.experimental import pallas as pl
from jax.experimental.pallas import tpu as pltpu
from jax.sharding import Mesh
from jax.sharding import PartitionSpec as P

DH = 128
NS_STEPS = 8
REFINE = 2
CHUNK = 256
VMEM = 16 * 2**20
SEQ = ("seq_0", "seq_1", "seq_2")
PLANE = ("seq_0", "seq_1")
CORE = "seq_2"

f32 = jnp.float32
bf16 = jnp.bfloat16


def mm(left, right):
    return jnp.dot(left, right, preferred_element_type=f32)


def mm_tn(left, right):
    return lax.dot_general(left, right, (((0,), (0,)), ((), ())), preferred_element_type=f32)


def mm_nt(left, right):
    return lax.dot_general(left, right, (((1,), (1,)), ((), ())), preferred_element_type=f32)


def split(x):
    high = x.astype(bf16)
    return high, (x - high.astype(f32)).astype(bf16)


def side(x):
    return jnp.concatenate(split(x), axis=1)


def doubled(x):
    x = side(x)
    return jnp.concatenate([x, x], axis=0)


def fold(x):
    return x[:, :DH] + x[:, DH:]


def eye():
    rows = lax.broadcasted_iota(jnp.int32, (DH, DH), 0)
    columns = lax.broadcasted_iota(jnp.int32, (DH, DH), 1)
    return (rows == columns).astype(f32)


def scaled_keys(key, gain):
    return (key.astype(f32) * gain).astype(bf16)


def gram_kernel(core_ref, gain_ref, k0_ref, v0_ref, k1_ref, v1_ref, keep_ref, send_ref):
    i = pl.program_id(0)
    core = core_ref[0]
    for k_ref, v_ref, out_ref, half in ((k0_ref, v0_ref, keep_ref, core), (k1_ref, v1_ref, send_ref, 1 - core)):
        k = scaled_keys(k_ref[...], gain_ref[half * pl.num_programs(0) + i])
        both = mm_tn(k, jnp.concatenate([k, v_ref[...]], axis=1))
        out_ref[0, 0] = both[:, :DH]
        out_ref[0, 1] = both[:, DH:]


def grams(core, gain, key, value):
    rows, width = key.shape
    half = width // DH // 2
    mine = pl.BlockSpec((rows, DH), lambda i, c: (0, i + half * c[0]))
    other = pl.BlockSpec((rows, DH), lambda i, c: (0, i + half * (1 - c[0])))
    out = pl.BlockSpec((1, 2, DH, DH), lambda i, c: (i, 0, 0, 0))
    shape = jax.ShapeDtypeStruct((half, 2, DH, DH), f32)
    return pl.pallas_call(
        gram_kernel,
        grid_spec=pltpu.PrefetchScalarGridSpec(
            num_scalar_prefetch=1,
            grid=(half,),
            in_specs=[pl.BlockSpec(memory_space=pltpu.SMEM), mine, mine, other, other],
            out_specs=[out, out],
        ),
        out_shape=[shape, shape],
        compiler_params=pltpu.CompilerParams(vmem_limit_bytes=VMEM),
        name="grams",
    )(core, gain, key, value, key, value)


def first_kernel(core_ref, gain_ref, k_ref, v_ref, gram_ref, cross_ref):
    heads = 2 * pl.num_programs(0)
    for a in range(2):
        h = lax.rem(2 * pl.program_id(0) + a + core_ref[0] * (heads // 2), heads)
        columns = slice(a * DH, (a + 1) * DH)
        k = scaled_keys(k_ref[:, columns], gain_ref[h])
        both = mm_tn(k, jnp.concatenate([k, v_ref[:, columns]], axis=1))
        gram_ref[a] = both[:, :DH]
        cross_ref[a] = both[:, DH:]


def first_grams(core, gain, key, value):
    steps = key.shape[1] // DH // 2
    block = pl.BlockSpec((CHUNK, 2 * DH), lambda i, c: (0, lax.rem(i + c[0] * (steps // 2), steps)))
    out = pl.BlockSpec((2, DH, DH), lambda i, c: (i, 0, 0))
    shape = jax.ShapeDtypeStruct((2 * steps, DH, DH), f32)
    return pl.pallas_call(
        first_kernel,
        grid_spec=pltpu.PrefetchScalarGridSpec(
            num_scalar_prefetch=1,
            grid=(steps,),
            in_specs=[pl.BlockSpec(memory_space=pltpu.SMEM), block, block],
            out_specs=[out, out],
        ),
        out_shape=[shape, shape],
        cost_estimate=pl.CostEstimate(flops=2 * 10**9, bytes_accessed=2 * 10**6, transcendentals=0),
        compiler_params=pltpu.CompilerParams(vmem_limit_bytes=VMEM),
        name="first_grams",
    )(core, gain, key, value)


def running_kernel(x_ref, o_ref):
    total = x_ref[0]
    o_ref[0] = jnp.zeros_like(total)
    for j in range(1, x_ref.shape[0]):
        o_ref[j] = total
        if j < x_ref.shape[0] - 1:
            total = total + x_ref[j]


def sums_before(pieces):
    return pl.pallas_call(
        running_kernel,
        out_shape=jax.ShapeDtypeStruct(pieces.shape, f32),
        in_specs=[pl.BlockSpec(memory_space=pltpu.VMEM)],
        out_specs=pl.BlockSpec(memory_space=pltpu.VMEM),
        compiler_params=pltpu.CompilerParams(vmem_limit_bytes=VMEM),
        name="sums_before",
    )(pieces)


def precond_kernel(core_ref, reg_ref, mine_ref, other_ref, keep_ref, send_ref, base_ref, y_ref):
    identity = eye()
    half = mine_ref.shape[0]
    inverse, approx, product = [], [], []
    for i in range(2 * half):
        first = i < half
        prior_ref, block_ref = (mine_ref, keep_ref) if first else (other_ref, send_ref)
        h = (core_ref[0] if first else 1 - core_ref[0]) * half + i % half
        base = identity * reg_ref[h] + prior_ref[i % half, 0]
        base_ref[i] = base
        end = base + block_ref[i % half, 0]
        squares = jnp.sum(jnp.sum(end * end, axis=0, keepdims=True), axis=1, keepdims=True)
        inv = 1.0 / jnp.sqrt(squares)
        z = end * inv
        inverse.append(inv)
        approx.append(2.0 * identity - z)
        product.append(2.0 * z - fold(mm(side(z), doubled(z))))
    for step in range(NS_STEPS - 2):
        for i in range(2 * half):
            both = jnp.concatenate([approx[i], product[i]], axis=0)
            both = 2.0 * both - fold(mm(side(both), doubled(product[i])))
            approx[i], product[i] = both[:DH], both[DH:]
    for i in range(2 * half):
        last = 2.0 * approx[i] - fold(mm(side(approx[i]), doubled(product[i])))
        y_ref[i] = last * inverse[i]


def preconditioners(core, reg, mine, other, keep, send):
    half = mine.shape[0]
    smem = pl.BlockSpec(memory_space=pltpu.SMEM)
    matrices = pl.BlockSpec((half, 1, DH, DH), lambda i: (0, 0, 0, 0))
    out = pl.BlockSpec((2 * half, DH, DH), lambda i: (0, 0, 0))
    shape = jax.ShapeDtypeStruct((2 * half, DH, DH), f32)
    return pl.pallas_call(
        precond_kernel,
        grid=(1,),
        in_specs=[smem, smem] + [matrices] * 4,
        out_specs=[out, out],
        out_shape=[shape, shape],
        compiler_params=pltpu.CompilerParams(vmem_limit_bytes=VMEM),
        name="preconditioners",
    )(core, reg, mine, other, keep, send)


def solve_kernel(core_ref, gain_ref, q_ref, k_ref, v_ref, y_ref, base_ref, gram_ref, mine_ref, other_ref, cross_ref, o_ref):
    step = pl.program_id(0)
    heads = 2 * pl.num_programs(0)
    shape = (CHUNK, CHUNK)
    causal = lax.broadcasted_iota(jnp.int32, shape, 0) >= lax.broadcasted_iota(jnp.int32, shape, 1)
    chains = []
    for a in range(2):
        h = lax.rem(2 * step + a + core_ref[0] * (heads // 2), heads)
        columns = slice(a * DH, (a + 1) * DH)
        k = scaled_keys(k_ref[:, columns], gain_ref[h])
        y = side(y_ref[a])
        cross = jnp.where(step < heads // 4, mine_ref[a, 0], other_ref[a, 0])
        for j in range(k.shape[0] // CHUNK):
            rows = slice(j * CHUNK, (j + 1) * CHUNK)
            base, prior = base_ref[a], cross
            if j:
                base, prior = base + gram_ref[a], prior + cross_ref[a]
            chains.append(
                dict(
                    at=(rows, columns), q=q_ref[rows, columns], k=k[rows], v=v_ref[rows, columns], y=y,
                    yy=jnp.concatenate([y, y], axis=0), base=doubled(base), prior=doubled(prior),
                )
            )
    for c in chains:
        c["s"] = fold(mm(c["q"], c["y"]))
    for repeat in range(REFINE):
        for c in chains:
            c["parts"] = split(c["s"])
            c["scores"] = jnp.where(causal, mm_nt(c["parts"][0], c["k"]), 0.0).astype(bf16)
        for c in chains:
            product = fold(mm(jnp.concatenate(c["parts"], axis=1), c["base"]))
            c["residual"] = c["q"].astype(f32) - product - mm(c["scores"], c["k"])
        for c in chains:
            c["s"] = c["s"] + fold(mm(side(c["residual"]), c["yy"]))
    for c in chains:
        parts = split(c["s"])
        scores = jnp.where(causal, mm_nt(parts[0], c["k"]), 0.0).astype(bf16)
        total = fold(mm(jnp.concatenate(parts, axis=1), c["prior"])) + mm(scores, c["v"])
        o_ref[c["at"]] = total.astype(bf16)


def solve(core, gain, query, key, value, y, base, gram, mine, other, cross):
    rows, width = query.shape
    steps = width // DH // 2
    smem = pl.BlockSpec(memory_space=pltpu.SMEM)
    wide = pl.BlockSpec((rows, 2 * DH), lambda i, c: (0, lax.rem(i + c[0] * (steps // 2), steps)))
    matrices = pl.BlockSpec((2, DH, DH), lambda i, c: (i, 0, 0))
    low = pl.BlockSpec((2, 1, DH, DH), lambda i, c: (jnp.minimum(i, steps // 2 - 1), 1, 0, 0))
    high = pl.BlockSpec((2, 1, DH, DH), lambda i, c: (jnp.maximum(i - steps // 2, 0), 1, 0, 0))
    return pl.pallas_call(
        solve_kernel,
        grid_spec=pltpu.PrefetchScalarGridSpec(
            num_scalar_prefetch=1,
            grid=(steps,),
            in_specs=[smem, wide, wide, wide, matrices, matrices, matrices, low, high, matrices],
            out_specs=wide,
        ),
        out_shape=jax.ShapeDtypeStruct((rows, width), bf16),
        compiler_params=pltpu.CompilerParams(vmem_limit_bytes=VMEM),
        name="solve",
    )(core, gain, query, key, value, y, base, gram, mine, other, cross)


def body(query_rows, key_rows, value_rows, key_gain, regularizer):
    place = lax.axis_index(CORE)
    core = place.astype(jnp.int32).reshape(1)
    swap = [(0, 1), (1, 0)]
    chips = lax.axis_size(PLANE)
    keep, send = grams(core, key_gain, key_rows, value_rows)
    received = lax.ppermute(send, CORE, swap)
    pieces = (keep + received).reshape(chips, -1, DH)
    pieces = lax.all_to_all(pieces, PLANE, 0, 0)
    first_gram, first_cross = first_grams(core, key_gain, key_rows, value_rows)
    before = lax.all_to_all(sums_before(pieces), PLANE, 0, 0).reshape(keep.shape)
    mine = before + jnp.where(place == 1, received, 0.0)
    other = lax.ppermute(before + jnp.where(place == 0, keep, 0.0), CORE, swap)
    base, y = preconditioners(core, regularizer, mine, other, keep, send)
    return solve(
        core, key_gain, query_rows, key_rows, value_rows, y, base, first_gram, mine, other, first_cross
    )


def solution(mesh):
    torus = Mesh(
        mesh.devices.reshape(8, 4, 2, mesh.shape["head"]), ("seq_0", "seq_1", "seq_2", "head")
    )
    in_specs = (P(SEQ, "head"), P(SEQ, "head"), P(SEQ, "head"), P("head"), P("head"))
    out_specs = P(SEQ, "head")
    return jax.shard_map(body, mesh=torus, in_specs=in_specs, out_specs=out_specs, check_vma=False)
```

time: 291 us -> 76.3 us (0.26)
  waiting for transfers between devices: 163 us -> 16.8 us
  matrix products: 81.8 us -> 0 us
  blocking collectives: 0 us -> 25.9 us
  Pallas kernels: 0 us -> 17.4 us
  other arithmetic: 15.2 us -> 0.2 us
  between operations: 13.4 us -> 0.07 us
  local copies, waits for them, and re-layouts: 16.4 us -> 3.75 us
  starting transfers between devices: 0.09 us -> 11.9 us
    all_gather x3 -> x0, waiting for transfers between devices: 163 us -> none  [prefix_by_axis(): pieces = lax.all_gather(subtotal, axis)]
    dot_general x90 -> x0, matrix products: 81.8 us -> none  [the longest x16 22.5 us: solve_head(): in_block = jnp.dot(scores, key_head, preferred_element_type=jnp.float32)]
    all_to_all x0 -> x1, blocking collectives: none -> 25.9 us  [body(): pieces = lax.all_to_all(pieces, PLANE, 0, 0)]
    pallas_call x0 -> x5, Pallas kernels: none -> 17.4 us  [the longest x1 9.57 us: solve(): pl.pallas_call(solve_kernel, grid_spec=pltpu.PrefetchScalarGridSpec(num_s...]
    all_to_all x0 -> x1, waiting for transfers between devices: none -> 15.2 us  [body(): lax.all_to_all(sums_before(pieces), PLANE, 0, 0).reshape(keep.shape)]
    add x3 -> x2, other arithmetic: 12.5 us -> 0.2 us  [the longest x1 0.12 us: body(): other = lax.ppermute(before + jnp.where(place == 0, keep, 0.0), CORE, swap)]
    dynamic_slice x16 -> x0, local copies, waits for them, and re-layouts: 8.29 us -> none  [body(): lax.map(solve_head, (jnp.transpose(query_split, (1, 0, 2)), jnp.transpose...]
    ppermute x0 -> x2, starting transfers between devices: none -> 6.94 us  [the longest x1 3.66 us: body(): other = lax.ppermute(before + jnp.where(place == 0, keep, 0.0), CORE, swap)]
  transfers between devices with their start and end apart: 3 -> 3, of which waited for: 3 -> 2; matrix products, arithmetic and copies ran while one was open for 1% -> 0% of each run, Pallas kernels for 0% -> 2%
where the time goes in v1:
time: 76.3 us; the launch traced here: 75.9 us
  blocking collectives  25.9 us (34%)
  Pallas kernels  17.4 us (23%)
  waiting for transfers between devices  16.8 us (22%)
  starting transfers between devices  11.9 us (16%)
  local copies, waits for them, and re-layouts  3.75 us (5%)
    all_to_all x1, blocking collectives, body(): pieces = lax.all_to_all(pieces, PLANE, 0, 0)  25.9 us
    all_to_all x1, waiting for transfers between devices, body(): lax.all_to_all(sums_before(pieces), PLANE, 0, 0).reshape(keep.shape)  15.2 us
    pallas_call x1, Pallas kernels, solve(): pl.pallas_call(solve_kernel, grid_spec=pltpu.PrefetchScalarGridSpec(num_s...  9.57 us
    all_to_all x1, starting transfers between devices, body(): lax.all_to_all(sums_before(pieces), PLANE, 0, 0).reshape(keep.shape)  4.93 us
    unnamed x14, local copies, waits for them, and re-layouts  3.75 us
    ppermute x1, starting transfers between devices, body(): other = lax.ppermute(before + jnp.where(place == 0, keep, 0.0), CORE, swap)  3.66 us
    ppermute x1, starting transfers between devices, body(): received = lax.ppermute(send, CORE, swap)  3.29 us
    pallas_call x1, Pallas kernels, preconditioners(): pl.pallas_call(precond_kernel, grid=(1,), in_specs=[smem, smem] + [matric...  2.98 us
  transfers between devices with their start and end apart: 3, of which 2 were waited for; matrix products, arithmetic and copies ran while one was open for 0% of the time, Pallas kernels for 2%

profile of v1, /device:TPU:1, one launch (start us, length us, event | category | flops | bytes accessed | tf_op | source)
XLA Modules:
  0.0 75.9 jit_solution(11076368522644479257)
XLA Ops:
  0.0 0.0 copy-start.5
  0.0 0.7 copy-done.5
  0.7 0.0 copy-start
  0.7 1.2 %copy-done = bf16[512,1024]{1,0:T(8,128)(2,1)S(1)} copy-done((bf16[512,1024]{1,0:T(8,128)(2,1)S(1)}, bf16[512,1024]{1,0:T(8,128)(2,1)}, u32[]{:S(2)}) %copy-start) | copy-done | bytes 1048600
  1.9 0.0 copy-start.2
  1.9 1.2 %copy-done.2 = bf16[512,1024]{1,0:T(8,128)(2,1)S(1)} copy-done((bf16[512,1024]{1,0:T(8,128)(2,1)S(1)}, bf16[512,1024]{1,0:T(8,128)(2,1)}, u32[]{:S(2)}) %copy-start.2) | copy-done | bytes 1048600
  3.1 2.3 %grams.1 = (f32[4,2,128,128]{3,2,1,0:T(8,128)S(1)}, f32[4,2,128,128]{3,2,1,0:T(8,128)S(1)}) custom-call(s32[1]{0:T(128)} %bitcast.core_ref, f32[8]{0:T(128)S(1)} %copy-done.5, bf16[512,1024]{1,0:T(8,128)(2,1)S(1)} %copy-done, bf16[512,1024]{1,0:T(8,128)(2,1)S(1)} %copy-done.2, bf16[512,1024]{1,0:T(8,128)(2,1)S(1)} %copy-done, bf16[512,1024]{1,0:T(8,128)(2,1)S(1)} %copy-done.2), custom_call_target="tpu_custom_call" | custom-call | tf_op jit(solution)/shard_map/grams/pallas_call | solution.py:80
  5.4 3.3 %collective-permute-start = (f32[4,2,128,128]{3,2,1,0:T(8,128)S(1)}, f32[4,2,128,128]{3,2,1,0:T(8,128)S(1)}, u32[]{:S(2)}, u32[]{:S(2)}) collective-permute-start(f32[4,2,128,128]{3,2,1,0:T(8,128)S(1)} %get-tuple-element.12.send_ref), channel_id=1, source_target_pairs={{0,4},{4,0},{1,5},{5,1},{2,6},{6,2},{3,7},{7,3},{8,12},{12,8},{9,1... | collective-permute-start | bytes 1572872 | tf_op jit(solution)/shard_map/ppermute | solution.py:258
  8.7 1.5 %collective-permute-done = f32[4,2,128,128]{3,2,1,0:T(8,128)S(1)} collective-permute-done((f32[4,2,128,128]{3,2,1,0:T(8,128)S(1)}, f32[4,2,128,128]{3,2,1,0:T(8,128)S(1)}, u32[]{:S(2)}, u32[]{:S(2)}) %collective-permute-start) | collective-permute-done | bytes 524320 | tf_op jit(solution)/shard_map/ppermute | solution.py:258
  10.2 0.1 add.9
  10.3 25.9 %all_to_all.10.x_ref = f32[32,32,128]{2,1,0:T(8,128)S(1)} all-to-all(f32[32,32,128]{2,1,0:T(8,128)S(1)} %bitcast.4), channel_id=1, replica_groups=mesh['seq_0'=8,'seq_1'=4,'seq_2'=2,'head'=4] {'seq_0','seq_1'}, dimensions={0} | all-to-all | bytes 1048576 | tf_op jit(solution)/shard_map/all_to_all | solution.py:260
  36.2 0.8 %sums_before.1 = f32[32,32,128]{2,1,0:T(8,128)} custom-call(f32[32,32,128]{2,1,0:T(8,128)S(1)} %all_to_all.10.x_ref), custom_call_target="tpu_custom_call" | custom-call | tf_op jit(solution)/shard_map/sums_before/pallas_call | solution.py:135
  37.0 4.9 %all-to-all-start.1 = ((f32[32,32,128]{2,1,0:T(8,128)}), f32[32,32,128]{2,1,0:T(8,128)S(1)}, u32[]{:S(2)}, u32[]{:S(2)}) async-start(f32[32,32,128]{2,1,0:T(8,128)} %sums_before.1), calls=%async_computation.1 | async-start | bytes 1048576 | tf_op jit(solution)/shard_map/all_to_all | solution.py:262
  42.0 15.2 %all-to-all-done.1 = f32[32,32,128]{2,1,0:T(8,128)S(1)} async-done(((f32[32,32,128]{2,1,0:T(8,128)}), f32[32,32,128]{2,1,0:T(8,128)S(1)}, u32[]{:S(2)}, u32[]{:S(2)}) %all-to-all-start.1) | async-done | bytes 524320 | tf_op jit(solution)/shard_map/all_to_all | solution.py:262
  57.2 0.0 copy-start.1
  57.2 0.0 copy-start.3
  57.2 0.1 select_add_fusion
  57.3 3.7 %collective-permute-start.1 = (f32[4,2,128,128]{3,2,1,0:T(8,128)S(1)}, f32[4,2,128,128]{3,2,1,0:T(8,128)S(1)}, u32[]{:S(2)}, u32[]{:S(2)}) collective-permute-start(f32[4,2,128,128]{3,2,1,0:T(8,128)S(1)} %get-tuple-element.17), channel_id=1, source_target_pairs={{0,4},{4,0},{1,5},{5,1},{2,6},{6,2},{3,7},{7,3},{8,12},{12,8},{9,1... | collective-permute-start | bytes 1572872 | tf_op jit(solution)/shard_map/ppermute | solution.py:264
  61.0 0.0 copy-done.1
  61.0 0.0 copy-done.3
  61.0 1.7 %first_grams.1 = (f32[8,128,128]{2,1,0:T(8,128)S(1)}, f32[8,128,128]{2,1,0:T(8,128)S(1)}) custom-call(s32[1]{0:T(128)} %bitcast.core_ref, f32[8]{0:T(128)S(1)} %copy-done.5, bf16[512,1024]{1,0:T(8,128)(2,1)S(1)} %copy-done.1, bf16[512,1024]{1,0:T(8,128)(2,1)S(1)} %copy-done.3), custom_call_target="tpu_custom_call" | custom-call | flops 2000000000 | bytes 2000000 | tf_op jit(solution)/shard_map/first_grams/pallas_call | solution.py:110
  62.7 0.0 copy-start.6
  62.7 0.0 collective-permute-done.1.other_ref
  62.7 0.6 copy-done.6
  63.4 0.0 copy-start.4
  63.4 3.0 %preconditioners.1 = (f32[8,128,128]{2,1,0:T(8,128)S(1)}, f32[8,128,128]{2,1,0:T(8,128)S(1)}) custom-call(s32[1]{0:T(128)} %bitcast.core_ref, f32[8]{0:T(128)S(1)} %copy-done.6, f32[4,2,128,128]{3,2,1,0:T(8,128)S(1)} %get-tuple-element.18.mine_ref, f32[4,2,128,128]{3,2,1,0:T(8,128)S(1)} %collective-permute-done.1.other_ref, ...), custom_call_target="tpu_custom_call" | custom-call | tf_op jit(solution)/shard_map/preconditioners/pallas_call | solution.py:178
  66.4 0.0 copy-done.4
  66.4 9.6 %solve.1 = bf16[512,1024]{1,0:T(8,128)(2,1)} custom-call(s32[1]{0:T(128)} %bitcast.core_ref, f32[8]{0:T(128)S(1)} %copy-done.5, bf16[512,1024]{1,0:T(8,128)(2,1)S(1)} %copy-done.4, bf16[512,1024]{1,0:T(8,128)(2,1)S(1)} %copy-done.1, bf16[512,1024]{1,0:T(8,128)(2,1)S(1)} %copy-done.3, f32[8,128,128]{2,1,0:T(8,128)S(1)} %get-tuple-element.13.y_ref, ...), custom_call_target="tpu_custom_call" | custom-call | tf_op jit(solution)/shard_map/solve/pallas_call | solution.py:238
Async XLA Ops:
  0.0 0.7 copy-start.5
  0.7 1.2 %copy-start = (bf16[512,1024]{1,0:T(8,128)(2,1)S(1)}, bf16[512,1024]{1,0:T(8,128)(2,1)}, u32[]{:S(2)}) copy-start(bf16[512,1024]{1,0:T(8,128)(2,1)} %k_ref.3) | copy-start | bytes 3145732
  1.9 1.2 %copy-start.2 = (bf16[512,1024]{1,0:T(8,128)(2,1)S(1)}, bf16[512,1024]{1,0:T(8,128)(2,1)}, u32[]{:S(2)}) copy-start(bf16[512,1024]{1,0:T(8,128)(2,1)} %v_ref.3) | copy-start | bytes 3145732
  5.4 4.8 %collective-permute-start = (f32[4,2,128,128]{3,2,1,0:T(8,128)S(1)}, f32[4,2,128,128]{3,2,1,0:T(8,128)S(1)}, u32[]{:S(2)}, u32[]{:S(2)}) collective-permute-start(f32[4,2,128,128]{3,2,1,0:T(8,128)S(1)} %get-tuple-element.12.send_ref), channel_id=1, source_target_pairs={{0,4},{4,0},{1,5},{5,1},{2,6},{6,2},{3,7},{7,3},{8,12},{12,8},{9,1... | collective-permute-start | bytes 1572872 | tf_op jit(solution)/shard_map/ppermute | solution.py:258
  37.0 20.2 %all-to-all-start.1 = ((f32[32,32,128]{2,1,0:T(8,128)}), f32[32,32,128]{2,1,0:T(8,128)S(1)}, u32[]{:S(2)}, u32[]{:S(2)}) async-start(f32[32,32,128]{2,1,0:T(8,128)} %sums_before.1), calls=%async_computation.1 | async-start | bytes 1048576 | tf_op jit(solution)/shard_map/all_to_all | solution.py:262
  57.2 3.8 %copy-start.1 = (bf16[512,1024]{1,0:T(8,128)(2,1)S(1)}, bf16[512,1024]{1,0:T(8,128)(2,1)}, u32[]{:S(2)}) copy-start(bf16[512,1024]{1,0:T(8,128)(2,1)} %k_ref.3) | copy-start | bytes 3145732
  57.2 3.8 %copy-start.3 = (bf16[512,1024]{1,0:T(8,128)(2,1)S(1)}, bf16[512,1024]{1,0:T(8,128)(2,1)}, u32[]{:S(2)}) copy-start(bf16[512,1024]{1,0:T(8,128)(2,1)} %v_ref.3) | copy-start | bytes 3145732
  57.3 5.4 %collective-permute-start.1 = (f32[4,2,128,128]{3,2,1,0:T(8,128)S(1)}, f32[4,2,128,128]{3,2,1,0:T(8,128)S(1)}, u32[]{:S(2)}, u32[]{:S(2)}) collective-permute-start(f32[4,2,128,128]{3,2,1,0:T(8,128)S(1)} %get-tuple-element.17), channel_id=1, source_target_pairs={{0,4},{4,0},{1,5},{5,1},{2,6},{6,2},{3,7},{7,3},{8,12},{12,8},{9,1... | collective-permute-start | bytes 1572872 | tf_op jit(solution)/shard_map/ppermute | solution.py:264
  62.7 0.7 copy-start.6
  63.4 3.0 %copy-start.4 = (bf16[512,1024]{1,0:T(8,128)(2,1)S(1)}, bf16[512,1024]{1,0:T(8,128)(2,1)}, u32[]{:S(2)}) copy-start(bf16[512,1024]{1,0:T(8,128)(2,1)} %q_ref.1) | copy-start | bytes 3145732

commit v2 on v1

v2 whole, which is shorter than its diff:
```python
import functools
import jax
import jax.numpy as jnp
from jax import lax
from jax.experimental import pallas as pl
from jax.experimental.pallas import tpu as pltpu
from jax.sharding import Mesh
from jax.sharding import PartitionSpec as P

DH = 128
NS_STEPS = 8
REFINE = 2
CHUNK = 256
VMEM = 16 * 2**20
SEQ = ("seq_0", "seq_1", "seq_2")
PLANE = ("seq_0", "seq_1")
CORE = "seq_2"

f32 = jnp.float32
bf16 = jnp.bfloat16


def mm(left, right):
    return jnp.dot(left, right, preferred_element_type=f32)


def mm_tn(left, right):
    return lax.dot_general(left, right, (((0,), (0,)), ((), ())), preferred_element_type=f32)


def mm_nt(left, right):
    return lax.dot_general(left, right, (((1,), (1,)), ((), ())), preferred_element_type=f32)


def split(x):
    high = x.astype(bf16)
    return high, (x - high.astype(f32)).astype(bf16)


def side(x):
    return jnp.concatenate(split(x), axis=1)


def doubled(x):
    x = side(x)
    return jnp.concatenate([x, x], axis=0)


def fold(x):
    return x[:, :DH] + x[:, DH:]


def eye():
    rows = lax.broadcasted_iota(jnp.int32, (DH, DH), 0)
    columns = lax.broadcasted_iota(jnp.int32, (DH, DH), 1)
    return (rows == columns).astype(f32)


def scaled_keys(key, gain):
    return (key.astype(f32) * gain).astype(bf16)


def in_hbm(*arrays):
    return [pltpu.with_memory_space_constraint(x, pltpu.HBM) for x in arrays]


def place_of(core_ref, step, heads):
    return lax.rem(step + core_ref[0] * (heads // 2), heads)


def gram_kernel(core_ref, gain_ref, reg_ref, k_ref, v_ref, keep_ref, send_ref, first_ref, scaled_ref, ridge_ref):
    step = pl.program_id(0)
    heads = 2 * pl.num_programs(0)
    both = []
    for a in range(2):
        h = place_of(core_ref, 2 * step + a, heads)
        columns = slice(a * DH, (a + 1) * DH)
        k = scaled_keys(k_ref[:, columns], gain_ref[h])
        scaled_ref[:, columns] = k
        ridge_ref[a] = jnp.full(ridge_ref.shape[1:], reg_ref[h])
        pair = jnp.concatenate([k, v_ref[:, columns]], axis=1)
        first = mm_tn(k[:CHUNK], pair[:CHUNK])
        first_ref[a, 0] = first[:, :DH]
        first_ref[a, 1] = first[:, DH:]
        both.append(first + mm_tn(k[CHUNK:], pair[CHUNK:]))

    def put(out_ref):
        for a in range(2):
            out_ref[a, 0] = both[a][:, :DH]
            out_ref[a, 1] = both[a][:, DH:]

    @pl.when(step < heads // 4)
    def _():
        put(keep_ref)

    @pl.when(step >= heads // 4)
    def _():
        put(send_ref)


def grams(core, gain, reg, key, value):
    gain, reg, key, value = in_hbm(gain, reg, key, value)
    rows, width = key.shape
    heads = width // DH
    steps = heads // 2
    smem = pl.BlockSpec(memory_space=pltpu.SMEM)
    wide = pl.BlockSpec((rows, 2 * DH), lambda i, c: (0, lax.rem(i + c[0] * (steps // 2), steps)))
    low = pl.BlockSpec((2, 2, DH, DH), lambda i, c: (jnp.minimum(i, steps // 2 - 1), 0, 0, 0))
    high = pl.BlockSpec((2, 2, DH, DH), lambda i, c: (jnp.maximum(i - steps // 2, 0), 0, 0, 0))
    every = pl.BlockSpec((2, 2, DH, DH), lambda i, c: (i, 0, 0, 0))
    half = jax.ShapeDtypeStruct((heads // 2, 2, DH, DH), f32)
    return pl.pallas_call(
        gram_kernel,
        grid_spec=pltpu.PrefetchScalarGridSpec(
            num_scalar_prefetch=1,
            grid=(steps,),
            in_specs=[smem, smem, wide, wide],
            out_specs=[low, high, every, wide, pl.BlockSpec((2, 8, DH), lambda i, c: (i, 0, 0))],
        ),
        out_shape=[
            half,
            half,
            jax.ShapeDtypeStruct((heads, 2, DH, DH), f32),
            jax.ShapeDtypeStruct((rows, width), bf16),
            jax.ShapeDtypeStruct((heads, 8, DH), f32),
        ],
        compiler_params=pltpu.CompilerParams(vmem_limit_bytes=VMEM),
        name="grams",
    )(core, gain, reg, key, value)


def running_kernel(x_ref, o_ref):
    total = x_ref[0]
    o_ref[0] = jnp.zeros_like(total)
    for j in range(1, x_ref.shape[0]):
        o_ref[j] = total
        if j < x_ref.shape[0] - 1:
            total = total + x_ref[j]


def sums_before(pieces):
    return pl.pallas_call(
        running_kernel,
        out_shape=jax.ShapeDtypeStruct(pieces.shape, f32),
        in_specs=[pl.BlockSpec(memory_space=pltpu.VMEM)],
        out_specs=pl.BlockSpec(memory_space=pltpu.VMEM),
        compiler_params=pltpu.CompilerParams(vmem_limit_bytes=VMEM),
        name="sums_before",
    )(pieces)


def precond_kernel(ridge_ref, prior_ref, block_ref, base_ref, y_ref):
    identity = eye()
    heads = range(prior_ref.shape[0])
    inverse, approx, product = [], [], []
    for i in heads:
        base = identity * ridge_ref[i, :1] + prior_ref[i, 0]
        base_ref[i] = base
        end = base + block_ref[i, 0]
        squares = jnp.sum(jnp.sum(end * end, axis=0, keepdims=True), axis=1, keepdims=True)
        inv = 1.0 / jnp.sqrt(squares)
        z = end * inv
        inverse.append(inv)
        approx.append(2.0 * identity - z)
        product.append(2.0 * z - fold(mm(side(z), doubled(z))))
    for step in range(NS_STEPS - 2):
        for i in heads:
            both = jnp.concatenate([approx[i], product[i]], axis=0)
            both = 2.0 * both - fold(mm(side(both), doubled(product[i])))
            approx[i], product[i] = both[:DH], both[DH:]
    for i in heads:
        last = 2.0 * approx[i] - fold(mm(side(approx[i]), doubled(product[i])))
        y_ref[i] = last * inverse[i]


def preconditioners(ridge, at, prior, block):
    half = prior.shape[0]
    matrices = pl.BlockSpec((half, 2, DH, DH), lambda i: (0, 0, 0, 0))
    out = pl.BlockSpec((half, DH, DH), lambda i: (0, 0, 0))
    shape = jax.ShapeDtypeStruct((half, DH, DH), f32)
    return pl.pallas_call(
        precond_kernel,
        grid=(1,),
        in_specs=[pl.BlockSpec((half, 8, DH), lambda i: (at, 0, 0)), matrices, matrices],
        out_specs=[out, out],
        out_shape=[shape, shape],
        compiler_params=pltpu.CompilerParams(vmem_limit_bytes=VMEM),
        cost_estimate=pl.CostEstimate(flops=10**9, bytes_accessed=2 * 10**6, transcendentals=0),
        name="preconditioners",
    )(ridge, prior, block)


def solve_kernel(core_ref, q_ref, k_ref, v_ref, first_ref, *refs):
    half_refs, o_ref = refs[:6], refs[6]
    low = pl.program_id(0) < pl.num_programs(0) // 2
    shape = (CHUNK, CHUNK)
    causal = lax.broadcasted_iota(jnp.int32, shape, 0) >= lax.broadcasted_iota(jnp.int32, shape, 1)
    chains = []
    for a in range(2):
        columns = slice(a * DH, (a + 1) * DH)
        y0, base, cross = [
            jnp.where(low, half_refs[n][a], half_refs[n + 1][a])
            if n < 4
            else jnp.where(low, half_refs[n][a, 0], half_refs[n + 1][a, 0])
            for n in (0, 2, 4)
        ]
        y = side(y0)
        for j in range(k_ref.shape[0] // CHUNK):
            rows = slice(j * CHUNK, (j + 1) * CHUNK)
            if j:
                base, cross = base + first_ref[a, 0], cross + first_ref[a, 1]
            chains.append(
                dict(
                    at=(rows, columns), q=q_ref[rows, columns], k=k_ref[rows, columns],
                    v=v_ref[rows, columns], y=y, yy=jnp.concatenate([y, y], axis=0),
                    base=doubled(base), prior=doubled(cross),
                )
            )
    for c in chains:
        c["s"] = fold(mm(c["q"], c["y"]))
    for repeat in range(REFINE):
        for c in chains:
            c["parts"] = split(c["s"])
            c["scores"] = jnp.where(causal, mm_nt(c["parts"][0], c["k"]), 0.0).astype(bf16)
        for c in chains:
            product = fold(mm(jnp.concatenate(c["parts"], axis=1), c["base"]))
            c["residual"] = c["q"].astype(f32) - product - mm(c["scores"], c["k"])
        for c in chains:
            c["s"] = c["s"] + fold(mm(side(c["residual"]), c["yy"]))
    for c in chains:
        parts = split(c["s"])
        scores = jnp.where(causal, mm_nt(parts[0], c["k"]), 0.0).astype(bf16)
        total = fold(mm(jnp.concatenate(parts, axis=1), c["prior"])) + mm(scores, c["v"])
        o_ref[c["at"]] = total.astype(bf16)


def solve(core, query, key, value, first, halves):
    rows, width = query.shape
    steps = width // DH // 2
    at_low = lambda i: jnp.minimum(i, steps // 2 - 1)
    at_high = lambda i: jnp.maximum(i - steps // 2, 0)
    wide = pl.BlockSpec((rows, 2 * DH), lambda i, c: (0, lax.rem(i + c[0] * (steps // 2), steps)))
    specs = []
    for at in (at_low, at_high) * 2:
        specs.append(pl.BlockSpec((2, DH, DH), lambda i, c, at=at: (at(i), 0, 0)))
    for at in (at_low, at_high):
        specs.append(pl.BlockSpec((2, 1, DH, DH), lambda i, c, at=at: (at(i), 1, 0, 0)))
    return pl.pallas_call(
        solve_kernel,
        grid_spec=pltpu.PrefetchScalarGridSpec(
            num_scalar_prefetch=1,
            grid=(steps,),
            in_specs=[wide, wide, wide, pl.BlockSpec((2, 2, DH, DH), lambda i, c: (i, 0, 0, 0))] + specs,
            out_specs=wide,
        ),
        out_shape=jax.ShapeDtypeStruct((rows, width), bf16),
        compiler_params=pltpu.CompilerParams(vmem_limit_bytes=VMEM),
        name="solve",
    )(core, query, key, value, first, *halves)


def exchange(x):
    return lax.all_to_all(x, PLANE, 0, 0)


def swapped(x):
    return lax.ppermute(x, CORE, [(0, 1), (1, 0)])


def body(query_rows, key_rows, value_rows, key_gain, regularizer):
    place = lax.axis_index(CORE)
    core = place.astype(jnp.int32).reshape(1)
    chips = lax.axis_size(PLANE)
    core, is_first, is_second = lax.optimization_barrier((core, place == 0, place == 1))
    keep, send, first, scaled, ridge = grams(core, key_gain, regularizer, key_rows, value_rows)
    received = swapped(send)
    pieces = exchange((keep + received).reshape(chips, -1, DH))
    before = exchange(sums_before(pieces)).reshape(keep.shape)
    mine = before + jnp.where(is_second, received, 0.0)
    other = swapped(before + jnp.where(is_first, keep, 0.0))
    base0, y0 = preconditioners(ridge, 0, mine, keep)
    base1, y1 = preconditioners(ridge, 1, other, send)
    return solve(
        core, query_rows, scaled, value_rows, first, (y0, y1, base0, base1, mine, other)
    )


def solution(mesh):
    torus = Mesh(
        mesh.devices.reshape(8, 4, 2, mesh.shape["head"]), ("seq_0", "seq_1", "seq_2", "head")
    )
    in_specs = (P(SEQ, "head"), P(SEQ, "head"), P(SEQ, "head"), P("head"), P("head"))
    out_specs = P(SEQ, "head")
    return jax.shard_map(body, mesh=torus, in_specs=in_specs, out_specs=out_specs, check_vma=False)
```

time: 76.3 us -> 71.2 us (0.933)
  blocking collectives: 25.9 us -> 45.9 us
  waiting for transfers between devices: 16.8 us -> 1.54 us
  starting transfers between devices: 11.9 us -> 6.94 us
  local copies, waits for them, and re-layouts: 3.75 us -> 0.01 us
  Pallas kernels: 17.4 us -> 16.3 us
    all_to_all x1 -> x2, blocking collectives: 25.9 us -> 45.9 us  [exchange(): return lax.all_to_all(x, PLANE, 0, 0)]
    all_to_all x1 -> x0, waiting for transfers between devices: 15.2 us -> none  [body(): lax.all_to_all(sums_before(pieces), PLANE, 0, 0).reshape(keep.shape)]
    all_to_all x1 -> x0, starting transfers between devices: 4.93 us -> none  [body(): lax.all_to_all(sums_before(pieces), PLANE, 0, 0).reshape(keep.shape)]
    unnamed x14 -> x4, local copies, waits for them, and re-layouts: 3.75 us -> 0.01 us
    pallas_call x1, Pallas kernels: 2.27 us -> 3.21 us  [grams(): pl.pallas_call(gram_kernel, grid_spec=pltpu.PrefetchScalarGridSpec(num_sc...]
    pallas_call x1, Pallas kernels: 0.83 us -> 0.04 us  [sums_before(): pl.pallas_call(running_kernel, out_shape=jax.ShapeDtypeStruct(pieces.shap...]
  transfers between devices with their start and end apart: 3 -> 2, of which waited for: 2 -> 1; matrix products, arithmetic and copies ran while one was open for 0% -> 0% of each run, Pallas kernels for 2% -> 3%
where the time goes in v2:
time: 71.2 us; the launch traced here: 71 us
  blocking collectives  45.9 us (64%)
  Pallas kernels  16.3 us (23%)
  starting transfers between devices  6.94 us (10%)
  waiting for transfers between devices  1.54 us (2%)
    all_to_all x2, blocking collectives, exchange(): return lax.all_to_all(x, PLANE, 0, 0)  45.9 us
    pallas_call x1, Pallas kernels, solve(): pl.pallas_call(solve_kernel, grid_spec=pltpu.PrefetchScalarGridSpec(num_s...  9.15 us
    ppermute x2, starting transfers between devices, swapped(): return lax.ppermute(x, CORE, [(0, 1), (1, 0)])  6.94 us
    pallas_call x2, Pallas kernels, preconditioners(): pl.pallas_call(precond_kernel, grid=(1,), in_specs=[pl.BlockSpec((half, 8...  3.95 us
    pallas_call x1, Pallas kernels, grams(): pl.pallas_call(gram_kernel, grid_spec=pltpu.PrefetchScalarGridSpec(num_sc...  3.21 us
    ppermute x2, waiting for transfers between devices, swapped(): return lax.ppermute(x, CORE, [(0, 1), (1, 0)])  1.54 us
  transfers between devices with their start and end apart: 2, of which 1 were waited for; matrix products, arithmetic and copies ran while one was open for 0% of the time, Pallas kernels for 3%

profile of v2, /device:TPU:1, one launch (start us, length us, event | category | flops | bytes accessed | tf_op | source)
XLA Modules:
  0.0 71.0 jit_solution(4449279133410511385)
XLA Ops:
  0.0 3.2 %grams.1 = (f32[4,2,128,128]{3,2,1,0:T(8,128)S(1)}, f32[4,2,128,128]{3,2,1,0:T(8,128)S(1)}, f32[8,2,128,128]{3,2,1,0:T(8,128)S(1)}, bf16[512,1024]{1,0:T(8,128)(2,1)S(1)}, f32[8,8,128]{2,1,0:T(8,128)S(1)}) custom-call(s32[1]{0:T(128)} %bitcast.core_ref, f32[8]{0:T(128)} %gain_ref.1, f32[8]{0:T(128)} %reg_ref.1, bf16[512,1024]{1,0:T(8,128)(2,1)} %k_ref.1, ...), custom_call_target="tpu_custom_call" | custom-call | tf_op jit(solution)/shard_map/grams/pallas_call | solution.py:112
  3.2 3.3 %collective-permute-start = (f32[4,2,128,128]{3,2,1,0:T(8,128)S(1)}, f32[4,2,128,128]{3,2,1,0:T(8,128)S(1)}, u32[]{:S(2)}, u32[]{:S(2)}) collective-permute-start(f32[4,2,128,128]{3,2,1,0:T(8,128)S(1)} %get-tuple-element.22.block_ref), channel_id=1, source_target_pairs={{0,4},{4,0},{1,5},{5,1},{2,6},{6,2},{3,7},{7,3},{8,12},{12,8},{9,1... | collective-permute-start | bytes 1572872 | tf_op jit(solution)/shard_map/ppermute | solution.py:267
  6.5 1.5 %collective-permute-done = f32[4,2,128,128]{3,2,1,0:T(8,128)S(1)} collective-permute-done((f32[4,2,128,128]{3,2,1,0:T(8,128)S(1)}, f32[4,2,128,128]{3,2,1,0:T(8,128)S(1)}, u32[]{:S(2)}, u32[]{:S(2)}) %collective-permute-start) | collective-permute-done | bytes 524320 | tf_op jit(solution)/shard_map/ppermute | solution.py:267
  8.0 0.1 add.9
  8.1 25.9 %all_to_all.10.x_ref = f32[32,32,128]{2,1,0:T(8,128)S(1)} all-to-all(f32[32,32,128]{2,1,0:T(8,128)S(1)} %bitcast.4), channel_id=1, replica_groups=mesh['seq_0'=8,'seq_1'=4,'seq_2'=2,'head'=4] {'seq_0','seq_1'}, dimensions={0} | all-to-all | bytes 1048576 | tf_op jit(solution)/shard_map/all_to_all | solution.py:263
  34.1 20.0 %all_to_all.11 = f32[32,32,128]{2,1,0:T(8,128)S(1)} all-to-all(f32[32,32,128]{2,1,0:T(8,128)S(1)} %sums_before.1), channel_id=1, replica_groups=mesh['seq_0'=8,'seq_1'=4,'seq_2'=2,'head'=4] {'seq_0','seq_1'}, dimensions={0} | all-to-all | bytes 1048576 | tf_op jit(solution)/shard_map/all_to_all | solution.py:263
  54.0 0.1 select_add_fusion
  54.2 3.7 %collective-permute-start.1 = (f32[4,2,128,128]{3,2,1,0:T(8,128)S(1)}, f32[4,2,128,128]{3,2,1,0:T(8,128)S(1)}, u32[]{:S(2)}, u32[]{:S(2)}) collective-permute-start(f32[4,2,128,128]{3,2,1,0:T(8,128)S(1)} %get-tuple-element.29), channel_id=1, source_target_pairs={{0,4},{4,0},{1,5},{5,1},{2,6},{6,2},{3,7},{7,3},{8,12},{12,8},{9,1... | collective-permute-start | bytes 1572872 | tf_op jit(solution)/shard_map/ppermute | solution.py:267
  57.8 2.0 %preconditioners.2 = (f32[4,128,128]{2,1,0:T(8,128)S(1)}, f32[4,128,128]{2,1,0:T(8,128)S(1)}) custom-call(f32[8,8,128]{2,1,0:T(8,128)S(1)} %get-tuple-element.20.ridge_ref, f32[4,2,128,128]{3,2,1,0:T(8,128)S(1)} %get-tuple-element.30.prior_ref.refs_4_, f32[4,2,128,128]{3,2,1,0:T(8,128)S(1)} %get-tuple-element.21.block_ref), custom_call_target="tpu_custom_call" | custom-call | flops 1000000000 | bytes 2000000 | tf_op jit(solution)/shard_map/preconditioners/pallas_call | solution.py:181
  59.8 0.0 copy-start
  59.8 0.0 copy-start.1
  59.8 0.0 collective-permute-done.1.prior_ref.refs_5_
  59.8 2.0 %preconditioners.3 = (f32[4,128,128]{2,1,0:T(8,128)S(1)}, f32[4,128,128]{2,1,0:T(8,128)S(1)}) custom-call(f32[8,8,128]{2,1,0:T(8,128)S(1)} %get-tuple-element.20.ridge_ref, f32[4,2,128,128]{3,2,1,0:T(8,128)S(1)} %collective-permute-done.1.prior_ref.refs_5_, f32[4,2,128,128]{3,2,1,0:T(8,128)S(1)} %get-tuple-element.22.block_ref), custom_call_target="tpu_custom_call" | custom-call | flops 1000000000 | bytes 2000000 | tf_op jit(solution)/shard_map/preconditioners/pallas_call | solution.py:181
  61.8 0.0 copy-done
  61.8 0.0 copy-done.1
  61.8 9.1 %solve.1 = bf16[512,1024]{1,0:T(8,128)(2,1)} custom-call(s32[1]{0:T(128)} %bitcast.core_ref, bf16[512,1024]{1,0:T(8,128)(2,1)S(1)} %copy-done.1, bf16[512,1024]{1,0:T(8,128)(2,1)S(1)} %get-tuple-element.18.k_ref, bf16[512,1024]{1,0:T(8,128)(2,1)S(1)} %copy-done, f32[8,2,128,128]{3,2,1,0:T(8,128)S(1)} %get-tuple-element.19.first_ref, ...), custom_call_target="tpu_custom_call" | custom-call | tf_op jit(solution)/shard_map/solve/pallas_call | solution.py:248
  (1 shorter events, 0.0 us)
Async XLA Ops:
  3.2 4.8 %collective-permute-start = (f32[4,2,128,128]{3,2,1,0:T(8,128)S(1)}, f32[4,2,128,128]{3,2,1,0:T(8,128)S(1)}, u32[]{:S(2)}, u32[]{:S(2)}) collective-permute-start(f32[4,2,128,128]{3,2,1,0:T(8,128)S(1)} %get-tuple-element.22.block_ref), channel_id=1, source_target_pairs={{0,4},{4,0},{1,5},{5,1},{2,6},{6,2},{3,7},{7,3},{8,12},{12,8},{9,1... | collective-permute-start | bytes 1572872 | tf_op jit(solution)/shard_map/ppermute | solution.py:267
  54.2 5.7 %collective-permute-start.1 = (f32[4,2,128,128]{3,2,1,0:T(8,128)S(1)}, f32[4,2,128,128]{3,2,1,0:T(8,128)S(1)}, u32[]{:S(2)}, u32[]{:S(2)}) collective-permute-start(f32[4,2,128,128]{3,2,1,0:T(8,128)S(1)} %get-tuple-element.29), channel_id=1, source_target_pairs={{0,4},{4,0},{1,5},{5,1},{2,6},{6,2},{3,7},{7,3},{8,12},{12,8},{9,1... | collective-permute-start | bytes 1572872 | tf_op jit(solution)/shard_map/ppermute | solution.py:267
  59.8 2.0 %copy-start = (bf16[512,1024]{1,0:T(8,128)(2,1)S(1)}, bf16[512,1024]{1,0:T(8,128)(2,1)}, u32[]{:S(2)}) copy-start(bf16[512,1024]{1,0:T(8,128)(2,1)} %v_ref.3) | copy-start | bytes 3145732
  59.8 2.0 %copy-start.1 = (bf16[512,1024]{1,0:T(8,128)(2,1)S(1)}, bf16[512,1024]{1,0:T(8,128)(2,1)}, u32[]{:S(2)}) copy-start(bf16[512,1024]{1,0:T(8,128)(2,1)} %q_ref.1) | copy-start | bytes 3145732

commit v3 on v2

--- a/solution.py
+++ b/solution.py
@@ -12,6 +12,7 @@
 REFINE = 2
 CHUNK = 256
 VMEM = 16 * 2**20
+PAIR = 400
 SEQ = ("seq_0", "seq_1", "seq_2")
 PLANE = ("seq_0", "seq_1")
 CORE = "seq_2"
@@ -68,7 +69,13 @@
     return lax.rem(step + core_ref[0] * (heads // 2), heads)
 
 
-def gram_kernel(core_ref, gain_ref, reg_ref, k_ref, v_ref, keep_ref, send_ref, first_ref, scaled_ref, ridge_ref):
+def triangles():
+    rows = lax.broadcasted_iota(jnp.int32, (DH, DH), 0)
+    columns = lax.broadcasted_iota(jnp.int32, (DH, DH), 1)
+    return rows <= columns, rows == columns
+
+
+def gram_kernel(core_ref, gain_ref, reg_ref, k_ref, v_ref, keep_ref, send_ref, local_ref, scaled_ref, ridge_ref):
     step = pl.program_id(0)
     heads = 2 * pl.num_programs(0)
     both = []
@@ -80,14 +87,20 @@
         ridge_ref[a] = jnp.full(ridge_ref.shape[1:], reg_ref[h])
         pair = jnp.concatenate([k, v_ref[:, columns]], axis=1)
         first = mm_tn(k[:CHUNK], pair[:CHUNK])
-        first_ref[a, 0] = first[:, :DH]
-        first_ref[a, 1] = first[:, DH:]
+        local_ref[a, 0] = first[:, :DH]
+        local_ref[a, 1] = first[:, DH:]
         both.append(first + mm_tn(k[CHUNK:], pair[CHUNK:]))
+        local_ref[a, 2] = both[a][:, :DH]
+    one, two = both[0][:, :DH], both[1][:, :DH]
+    above, on = triangles()
+    packed = jnp.where(above, one, two)
+    diagonal = jnp.sum(jnp.where(on, two, 0.0), axis=0, keepdims=True)
 
     def put(out_ref):
         for a in range(2):
-            out_ref[a, 0] = both[a][:, :DH]
-            out_ref[a, 1] = both[a][:, DH:]
+            out_ref[0, a * DH : (a + 1) * DH] = both[a][:, DH:]
+        out_ref[0, 2 * DH : 3 * DH] = packed
+        out_ref[0, 3 * DH :] = jnp.broadcast_to(diagonal, (PAIR - 3 * DH, DH))
 
     @pl.when(step < heads // 4)
     def _():
@@ -105,22 +118,27 @@
     steps = heads // 2
     smem = pl.BlockSpec(memory_space=pltpu.SMEM)
     wide = pl.BlockSpec((rows, 2 * DH), lambda i, c: (0, lax.rem(i + c[0] * (steps // 2), steps)))
-    low = pl.BlockSpec((2, 2, DH, DH), lambda i, c: (jnp.minimum(i, steps // 2 - 1), 0, 0, 0))
-    high = pl.BlockSpec((2, 2, DH, DH), lambda i, c: (jnp.maximum(i - steps // 2, 0), 0, 0, 0))
-    every = pl.BlockSpec((2, 2, DH, DH), lambda i, c: (i, 0, 0, 0))
-    half = jax.ShapeDtypeStruct((heads // 2, 2, DH, DH), f32)
+    low = pl.BlockSpec((1, PAIR, DH), lambda i, c: (jnp.minimum(i, steps // 2 - 1), 0, 0))
+    high = pl.BlockSpec((1, PAIR, DH), lambda i, c: (jnp.maximum(i - steps // 2, 0), 0, 0))
+    slabs = jax.ShapeDtypeStruct((steps // 2, PAIR, DH), f32)
     return pl.pallas_call(
         gram_kernel,
         grid_spec=pltpu.PrefetchScalarGridSpec(
             num_scalar_prefetch=1,
             grid=(steps,),
             in_specs=[smem, smem, wide, wide],
-            out_specs=[low, high, every, wide, pl.BlockSpec((2, 8, DH), lambda i, c: (i, 0, 0))],
+            out_specs=[
+                low,
+                high,
+                pl.BlockSpec((2, 3, DH, DH), lambda i, c: (i, 0, 0, 0)),
+                wide,
+                pl.BlockSpec((2, 8, DH), lambda i, c: (i, 0, 0)),
+            ],
         ),
         out_shape=[
-            half,
-            half,
-            jax.ShapeDtypeStruct((heads, 2, DH, DH), f32),
+            slabs,
+            slabs,
+            jax.ShapeDtypeStruct((heads, 3, DH, DH), f32),
             jax.ShapeDtypeStruct((rows, width), bf16),
             jax.ShapeDtypeStruct((heads, 8, DH), f32),
         ],
@@ -149,14 +167,22 @@
     )(pieces)
 
 
-def precond_kernel(ridge_ref, prior_ref, block_ref, base_ref, y_ref):
+def precond_kernel(ridge_ref, prior_ref, local_ref, base_ref, y_ref):
     identity = eye()
-    heads = range(prior_ref.shape[0])
+    above, on = triangles()
+    heads = range(local_ref.shape[0])
+    priors = []
+    for pair in range(prior_ref.shape[0]):
+        packed = prior_ref[pair, 2 * DH : 3 * DH]
+        turned = packed.T
+        diagonal = prior_ref[pair, 3 * DH : 3 * DH + 1]
+        priors.append(jnp.where(above, packed, turned))
+        priors.append(jnp.where(on, diagonal, jnp.where(above, turned, packed)))
     inverse, approx, product = [], [], []
     for i in heads:
-        base = identity * ridge_ref[i, :1] + prior_ref[i, 0]
+        base = identity * ridge_ref[i, :1] + priors[i]
         base_ref[i] = base
-        end = base + block_ref[i, 0]
+        end = base + local_ref[i, 0]
         squares = jnp.sum(jnp.sum(end * end, axis=0, keepdims=True), axis=1, keepdims=True)
         inv = 1.0 / jnp.sqrt(squares)
         z = end * inv
@@ -173,24 +199,27 @@
         y_ref[i] = last * inverse[i]
 
 
-def preconditioners(ridge, at, prior, block):
-    half = prior.shape[0]
-    matrices = pl.BlockSpec((half, 2, DH, DH), lambda i: (0, 0, 0, 0))
+def preconditioners(ridge, at, prior, local):
+    half = 2 * prior.shape[0]
     out = pl.BlockSpec((half, DH, DH), lambda i: (0, 0, 0))
     shape = jax.ShapeDtypeStruct((half, DH, DH), f32)
     return pl.pallas_call(
         precond_kernel,
         grid=(1,),
-        in_specs=[pl.BlockSpec((half, 8, DH), lambda i: (at, 0, 0)), matrices, matrices],
+        in_specs=[
+            pl.BlockSpec((half, 8, DH), lambda i: (at, 0, 0)),
+            pl.BlockSpec(prior.shape, lambda i: (0, 0, 0)),
+            pl.BlockSpec((half, 1, DH, DH), lambda i: (at, 2, 0, 0)),
+        ],
         out_specs=[out, out],
         out_shape=[shape, shape],
         compiler_params=pltpu.CompilerParams(vmem_limit_bytes=VMEM),
         cost_estimate=pl.CostEstimate(flops=10**9, bytes_accessed=2 * 10**6, transcendentals=0),
         name="preconditioners",
-    )(ridge, prior, block)
-
-
-def solve_kernel(core_ref, q_ref, k_ref, v_ref, first_ref, *refs):
+    )(ridge, prior, local)
+
+
+def solve_kernel(core_ref, q_ref, k_ref, v_ref, local_ref, *refs):
     half_refs, o_ref = refs[:6], refs[6]
     low = pl.program_id(0) < pl.num_programs(0) // 2
     shape = (CHUNK, CHUNK)
@@ -198,17 +227,13 @@
     chains = []
     for a in range(2):
         columns = slice(a * DH, (a + 1) * DH)
-        y0, base, cross = [
-            jnp.where(low, half_refs[n][a], half_refs[n + 1][a])
-            if n < 4
-            else jnp.where(low, half_refs[n][a, 0], half_refs[n + 1][a, 0])
-            for n in (0, 2, 4)
-        ]
-        y = side(y0)
+        y = side(jnp.where(low, half_refs[0][a], half_refs[1][a]))
+        base = jnp.where(low, half_refs[2][a], half_refs[3][a])
+        cross = jnp.where(low, half_refs[4][0, columns], half_refs[5][0, columns])
         for j in range(k_ref.shape[0] // CHUNK):
             rows = slice(j * CHUNK, (j + 1) * CHUNK)
             if j:
-                base, cross = base + first_ref[a, 0], cross + first_ref[a, 1]
+                base, cross = base + local_ref[a, 0], cross + local_ref[a, 1]
             chains.append(
                 dict(
                     at=(rows, columns), q=q_ref[rows, columns], k=k_ref[rows, columns],
@@ -234,7 +259,7 @@
         o_ref[c["at"]] = total.astype(bf16)
 
 
-def solve(core, query, key, value, first, halves):
+def solve(core, query, key, value, local, halves):
     rows, width = query.shape
     steps = width // DH // 2
     at_low = lambda i: jnp.minimum(i, steps // 2 - 1)
@@ -244,7 +269,7 @@
     for at in (at_low, at_high) * 2:
         specs.append(pl.BlockSpec((2, DH, DH), lambda i, c, at=at: (at(i), 0, 0)))
     for at in (at_low, at_high):
-        specs.append(pl.BlockSpec((2, 1, DH, DH), lambda i, c, at=at: (at(i), 1, 0, 0)))
+        specs.append(pl.BlockSpec((1, 2 * DH, DH), lambda i, c, at=at: (at(i), 0, 0)))
     return pl.pallas_call(
         solve_kernel,
         grid_spec=pltpu.PrefetchScalarGridSpec(
@@ -256,7 +281,7 @@
         out_shape=jax.ShapeDtypeStruct((rows, width), bf16),
         compiler_params=pltpu.CompilerParams(vmem_limit_bytes=VMEM),
         name="solve",
-    )(core, query, key, value, first, *halves)
+    )(core, query, key, value, local, *halves)
 
 
 def exchange(x):
@@ -272,16 +297,16 @@
     core = place.astype(jnp.int32).reshape(1)
     chips = lax.axis_size(PLANE)
     core, is_first, is_second = lax.optimization_barrier((core, place == 0, place == 1))
-    keep, send, first, scaled, ridge = grams(core, key_gain, regularizer, key_rows, value_rows)
+    keep, send, local, scaled, ridge = grams(core, key_gain, regularizer, key_rows, value_rows)
     received = swapped(send)
-    pieces = exchange((keep + received).reshape(chips, -1, DH))
+    pieces = exchange((keep + received).reshape(chips, 1, -1))
     before = exchange(sums_before(pieces)).reshape(keep.shape)
     mine = before + jnp.where(is_second, received, 0.0)
     other = swapped(before + jnp.where(is_first, keep, 0.0))
-    base0, y0 = preconditioners(ridge, 0, mine, keep)
-    base1, y1 = preconditioners(ridge, 1, other, send)
+    base0, y0 = preconditioners(ridge, 0, mine, local)
+    base1, y1 = preconditioners(ridge, 1, other, local)
     return solve(
-        core, query_rows, scaled, value_rows, first, (y0, y1, base0, base1, mine, other)
+        core, query_rows, scaled, value_rows, local, (y0, y1, base0, base1, mine, other)
     )
 
 

time: 71.2 us -> 66.9 us (0.940)
  blocking collectives: 45.9 us -> 41.5 us
    all_to_all x2, blocking collectives: 45.9 us -> 41.5 us  [exchange(): return lax.all_to_all(x, PLANE, 0, 0)]
where the time goes in v3:
time: 66.9 us; the launch traced here: 66.7 us
  blocking collectives  41.5 us (62%)
  Pallas kernels  16.7 us (25%)
  starting transfers between devices  6.94 us (10%)
  waiting for transfers between devices  1.38 us (2%)
    all_to_all x2, blocking collectives, exchange(): return lax.all_to_all(x, PLANE, 0, 0)  41.5 us
    pallas_call x1, Pallas kernels, solve(): pl.pallas_call(solve_kernel, grid_spec=pltpu.PrefetchScalarGridSpec(num_s...  9.12 us
    ppermute x2, starting transfers between devices, swapped(): return lax.ppermute(x, CORE, [(0, 1), (1, 0)])  6.94 us
    pallas_call x2, Pallas kernels, preconditioners(): pl.pallas_call(precond_kernel, grid=(1,), in_specs=[pl.BlockSpec((half, 8...  4.28 us
    pallas_call x1, Pallas kernels, grams(): pl.pallas_call(gram_kernel, grid_spec=pltpu.PrefetchScalarGridSpec(num_sc...  3.23 us
    ppermute x2, waiting for transfers between devices, swapped(): return lax.ppermute(x, CORE, [(0, 1), (1, 0)])  1.38 us
  transfers between devices with their start and end apart: 2, of which 1 were waited for; matrix products, arithmetic and copies ran while one was open for 0% of the time, Pallas kernels for 3%

profile of v3, /device:TPU:1, one launch (start us, length us, event | category | flops | bytes accessed | tf_op | source)
XLA Modules:
  0.0 66.7 jit_solution(6174640860914078453)
XLA Ops:
  0.0 3.2 %grams.1 = (f32[2,400,128]{2,1,0:T(8,128)S(1)}, f32[2,400,128]{2,1,0:T(8,128)S(1)}, f32[8,3,128,128]{3,2,1,0:T(8,128)S(1)}, bf16[512,1024]{1,0:T(8,128)(2,1)S(1)}, f32[8,8,128]{2,1,0:T(8,128)S(1)}) custom-call(s32[1]{0:T(128)} %bitcast.core_ref, f32[8]{0:T(128)} %gain_ref.1, f32[8]{0:T(128)} %reg_ref.1, bf16[512,1024]{1,0:T(8,128)(2,1)} %k_ref.1, ...), custom_call_target="tpu_custom_call" | custom-call | tf_op jit(solution)/shard_map/grams/pallas_call | solution.py:124
  3.2 3.3 %collective-permute-start = (f32[2,400,128]{2,1,0:T(8,128)S(1)}, f32[2,400,128]{2,1,0:T(8,128)S(1)}, u32[]{:S(2)}, u32[]{:S(2)}) collective-permute-start(f32[2,400,128]{2,1,0:T(8,128)S(1)} %get-tuple-element.22), channel_id=1, source_target_pairs={{0,4},{4,0},{1,5},{5,1},{2,6},{6,2},{3,7},{7,3},{8,12},{12,8},{9,1... | collective-permute-start | bytes 1228808 | tf_op jit(solution)/shard_map/ppermute | solution.py:292
  6.5 1.4 %collective-permute-done = f32[2,400,128]{2,1,0:T(8,128)S(1)} collective-permute-done((f32[2,400,128]{2,1,0:T(8,128)S(1)}, f32[2,400,128]{2,1,0:T(8,128)S(1)}, u32[]{:S(2)}, u32[]{:S(2)}) %collective-permute-start) | collective-permute-done | bytes 409632 | tf_op jit(solution)/shard_map/ppermute | solution.py:292
  7.9 0.1 add.9
  8.0 23.5 %all_to_all.10.x_ref = f32[32,1,3200]{2,1,0:T(1,128)S(1)} all-to-all(f32[32,1,3200]{2,1,0:T(1,128)S(1)} %bitcast.7), channel_id=1, replica_groups=mesh['seq_0'=8,'seq_1'=4,'seq_2'=2,'head'=4] {'seq_0','seq_1'}, dimensions={0} | all-to-all | bytes 819200 | tf_op jit(solution)/shard_map/all_to_all | solution.py:288
  31.5 18.0 %all_to_all.11 = f32[32,1,3200]{2,1,0:T(1,128)S(1)} all-to-all(f32[32,1,3200]{2,1,0:T(1,128)S(1)} %sums_before.1), channel_id=1, replica_groups=mesh['seq_0'=8,'seq_1'=4,'seq_2'=2,'head'=4] {'seq_0','seq_1'}, dimensions={0} | all-to-all | bytes 819200 | tf_op jit(solution)/shard_map/all_to_all | solution.py:288
  49.5 0.1 bitcast_add_fusion
  49.6 3.7 %collective-permute-start.1 = (f32[2,400,128]{2,1,0:T(8,128)S(1)}, f32[2,400,128]{2,1,0:T(8,128)S(1)}, u32[]{:S(2)}, u32[]{:S(2)}) collective-permute-start(f32[2,400,128]{2,1,0:T(8,128)S(1)} %get-tuple-element.29), channel_id=1, source_target_pairs={{0,4},{4,0},{1,5},{5,1},{2,6},{6,2},{3,7},{7,3},{8,12},{12,8},{9,1... | collective-permute-start | bytes 1228808 | tf_op jit(solution)/shard_map/ppermute | solution.py:292
  53.2 2.1 %preconditioners.2 = (f32[4,128,128]{2,1,0:T(8,128)S(1)}, f32[4,128,128]{2,1,0:T(8,128)S(1)}) custom-call(f32[8,8,128]{2,1,0:T(8,128)S(1)} %get-tuple-element.20.ridge_ref, f32[2,400,128]{2,1,0:T(8,128)S(1)} %get-tuple-element.30.prior_ref.refs_4_, f32[8,3,128,128]{3,2,1,0:T(8,128)S(1)} %get-tuple-element.19.local_ref), custom_call_target="tpu_custom_call" | custom-call | flops 1000000000 | bytes 2000000 | tf_op jit(solution)/shard_map/preconditioners/pallas_call | solution.py:206
  55.4 0.0 copy-start
  55.4 0.0 copy-start.1
  55.4 0.0 collective-permute-done.1.prior_ref.refs_5_
  55.4 2.1 %preconditioners.3 = (f32[4,128,128]{2,1,0:T(8,128)S(1)}, f32[4,128,128]{2,1,0:T(8,128)S(1)}) custom-call(f32[8,8,128]{2,1,0:T(8,128)S(1)} %get-tuple-element.20.ridge_ref, f32[2,400,128]{2,1,0:T(8,128)S(1)} %collective-permute-done.1.prior_ref.refs_5_, f32[8,3,128,128]{3,2,1,0:T(8,128)S(1)} %get-tuple-element.19.local_ref), custom_call_target="tpu_custom_call" | custom-call | flops 1000000000 | bytes 2000000 | tf_op jit(solution)/shard_map/preconditioners/pallas_call | solution.py:206
  57.5 0.0 copy-done
  57.6 0.0 copy-done.1
  57.6 9.1 %solve.1 = bf16[512,1024]{1,0:T(8,128)(2,1)} custom-call(s32[1]{0:T(128)} %bitcast.core_ref, bf16[512,1024]{1,0:T(8,128)(2,1)S(1)} %copy-done.1, bf16[512,1024]{1,0:T(8,128)(2,1)S(1)} %get-tuple-element.18.k_ref, bf16[512,1024]{1,0:T(8,128)(2,1)S(1)} %copy-done, f32[8,3,128,128]{3,2,1,0:T(8,128)S(1)} %get-tuple-element.19.local_ref, ...), custom_call_target="tpu_custom_call" | custom-call | tf_op jit(solution)/shard_map/solve/pallas_call | solution.py:273
  (1 shorter events, 0.0 us)
Async XLA Ops:
  3.2 4.7 %collective-permute-start = (f32[2,400,128]{2,1,0:T(8,128)S(1)}, f32[2,400,128]{2,1,0:T(8,128)S(1)}, u32[]{:S(2)}, u32[]{:S(2)}) collective-permute-start(f32[2,400,128]{2,1,0:T(8,128)S(1)} %get-tuple-element.22), channel_id=1, source_target_pairs={{0,4},{4,0},{1,5},{5,1},{2,6},{6,2},{3,7},{7,3},{8,12},{12,8},{9,1... | collective-permute-start | bytes 1228808 | tf_op jit(solution)/shard_map/ppermute | solution.py:292
  49.6 5.8 %collective-permute-start.1 = (f32[2,400,128]{2,1,0:T(8,128)S(1)}, f32[2,400,128]{2,1,0:T(8,128)S(1)}, u32[]{:S(2)}, u32[]{:S(2)}) collective-permute-start(f32[2,400,128]{2,1,0:T(8,128)S(1)} %get-tuple-element.29), channel_id=1, source_target_pairs={{0,4},{4,0},{1,5},{5,1},{2,6},{6,2},{3,7},{7,3},{8,12},{12,8},{9,1... | collective-permute-start | bytes 1228808 | tf_op jit(solution)/shard_map/ppermute | solution.py:292
  55.4 2.2 %copy-start = (bf16[512,1024]{1,0:T(8,128)(2,1)S(1)}, bf16[512,1024]{1,0:T(8,128)(2,1)}, u32[]{:S(2)}) copy-start(bf16[512,1024]{1,0:T(8,128)(2,1)} %v_ref.3) | copy-start | bytes 3145732
  55.4 2.2 %copy-start.1 = (bf16[512,1024]{1,0:T(8,128)(2,1)S(1)}, bf16[512,1024]{1,0:T(8,128)(2,1)}, u32[]{:S(2)}) copy-start(bf16[512,1024]{1,0:T(8,128)(2,1)} %q_ref.1) | copy-start | bytes 3145732

commit v4 on v3

--- a/solution.py
+++ b/solution.py
@@ -11,7 +11,7 @@
 NS_STEPS = 8
 REFINE = 2
 CHUNK = 256
-VMEM = 16 * 2**20
+VMEM = 20 * 2**20
 PAIR = 400
 SEQ = ("seq_0", "seq_1", "seq_2")
 PLANE = ("seq_0", "seq_1")
@@ -167,121 +167,237 @@
     )(pieces)
 
 
-def precond_kernel(ridge_ref, prior_ref, local_ref, base_ref, y_ref):
-    identity = eye()
-    above, on = triangles()
+def newton_schulz(ridge_ref, prior_ref, local_ref, base_ref, y_ref):
     heads = range(local_ref.shape[0])
-    priors = []
-    for pair in range(prior_ref.shape[0]):
-        packed = prior_ref[pair, 2 * DH : 3 * DH]
-        turned = packed.T
-        diagonal = prior_ref[pair, 3 * DH : 3 * DH + 1]
-        priors.append(jnp.where(above, packed, turned))
-        priors.append(jnp.where(on, diagonal, jnp.where(above, turned, packed)))
-    inverse, approx, product = [], [], []
-    for i in heads:
-        base = identity * ridge_ref[i, :1] + priors[i]
-        base_ref[i] = base
-        end = base + local_ref[i, 0]
-        squares = jnp.sum(jnp.sum(end * end, axis=0, keepdims=True), axis=1, keepdims=True)
-        inv = 1.0 / jnp.sqrt(squares)
-        z = end * inv
-        inverse.append(inv)
-        approx.append(2.0 * identity - z)
-        product.append(2.0 * z - fold(mm(side(z), doubled(z))))
-    for step in range(NS_STEPS - 2):
+    inverse, approx, product = {}, {}, {}
+
+    def begin():
+        identity = eye()
+        above, on = triangles()
+        priors = []
+        for pair in range(prior_ref.shape[0]):
+            packed = prior_ref[pair, 2 * DH : 3 * DH]
+            turned = packed.T
+            diagonal = prior_ref[pair, 3 * DH : 3 * DH + 1]
+            priors.append(jnp.where(above, packed, turned))
+            priors.append(jnp.where(on, diagonal, jnp.where(above, turned, packed)))
+        for i in heads:
+            base = identity * ridge_ref[i, :1] + priors[i]
+            base_ref[i] = base
+            end = base + local_ref[i, 2]
+            squares = jnp.sum(jnp.sum(end * end, axis=0, keepdims=True), axis=1, keepdims=True)
+            inverse[i] = 1.0 / jnp.sqrt(squares)
+            z = end * inverse[i]
+            approx[i] = 2.0 * identity - z
+            product[i] = 2.0 * z - fold(mm(side(z), doubled(z)))
+
+    def step():
         for i in heads:
             both = jnp.concatenate([approx[i], product[i]], axis=0)
             both = 2.0 * both - fold(mm(side(both), doubled(product[i])))
             approx[i], product[i] = both[:DH], both[DH:]
-    for i in heads:
-        last = 2.0 * approx[i] - fold(mm(side(approx[i]), doubled(product[i])))
-        y_ref[i] = last * inverse[i]
-
-
-def preconditioners(ridge, at, prior, local):
-    half = 2 * prior.shape[0]
-    out = pl.BlockSpec((half, DH, DH), lambda i: (0, 0, 0))
-    shape = jax.ShapeDtypeStruct((half, DH, DH), f32)
+
+    def end():
+        for i in heads:
+            last = 2.0 * approx[i] - fold(mm(side(approx[i]), doubled(product[i])))
+            y_ref[i] = last * inverse[i]
+
+    return [begin] + [step] * (NS_STEPS - 2) + [end]
+
+
+def diagonal_blocks(two):
+    zero = jnp.zeros((DH, DH), two.dtype)
+    upper = jnp.concatenate([two[:, :DH], zero], axis=1)
+    lower = jnp.concatenate([zero, two[:, DH:]], axis=1)
+    return jnp.concatenate([upper, lower], axis=0)
+
+
+def halves_of(x):
+    return x[:, :DH], x[:, DH:]
+
+
+def beside(parts):
+    high, low = (halves_of(x) for x in parts)
+    return [jnp.concatenate([high[a], low[a]], axis=1) for a in range(2)]
+
+
+def solving(half, q_ref, k_ref, v_ref, y_ref, base_ref, prior_ref, local_ref, o_ref):
+    rows_in = q_ref.shape[0]
+    width = q_ref.shape[1] // 2
+    groups, weights = [], {}
+
+    def begin():
+        shape = (CHUNK, 2 * DH)
+        columns = lax.rem(lax.broadcasted_iota(jnp.int32, shape, 1), DH)
+        weights["causal"] = lax.broadcasted_iota(jnp.int32, shape, 0) >= columns
+        for p in range(width // (2 * DH)):
+            inside = slice(2 * p * DH, 2 * (p + 1) * DH)
+            columns = pl.ds(pl.multiple_of(half * width + 2 * p * DH, 2 * DH), 2 * DH)
+            group = []
+            for a in range(2):
+                y = side(y_ref[2 * p + a])
+                weights[p, a] = y, jnp.concatenate([y, y], axis=0)
+            for j in range(rows_in // CHUNK):
+                rows = slice(j * CHUNK, (j + 1) * CHUNK)
+                k, v = k_ref[rows, columns], v_ref[rows, columns]
+                base, prior = [], []
+                for a in range(2):
+                    h = 2 * p + a
+                    b, c = base_ref[h], prior_ref[p, a * DH : (a + 1) * DH]
+                    base.append(doubled(b + local_ref[h, 0] if j else b))
+                    prior.append(doubled(c + local_ref[h, 1] if j else c))
+                blocks = lambda x: [diagonal_blocks(x[i * DH : (i + 1) * DH]) for i in range(CHUNK // DH)]
+                group.append(dict(at=(rows, inside), q=q_ref[rows, columns], k=blocks(k), v=blocks(v), base=base, prior=prior))
+            groups.append(group)
+        through("s", 0, lambda c: halves_of(c["q"]))
+
+    def through(key, which, rows_of):
+        for p, group in enumerate(groups):
+            parts = [rows_of(c) for c in group]
+            out = []
+            for a in range(2):
+                rows = jnp.concatenate([x[a] for x in parts], axis=0)
+                out.append(fold(mm(rows, weights[p, a][which])))
+            for n, c in enumerate(group):
+                c[key] = jnp.concatenate([x[n * CHUNK : (n + 1) * CHUNK] for x in out], axis=1)
+
+    def each(function):
+        def run():
+            for group in groups:
+                for c in group:
+                    function(c)
+
+        return run
+
+    def score(c):
+        c["parts"] = split(c["s"])
+        high = c["parts"][0]
+        c["scores"] = []
+        for i, k in enumerate(c["k"]):
+            scores = mm_nt(high[i * DH :], k)
+            causal = weights["causal"][: CHUNK - i * DH]
+            c["scores"].append(jnp.where(causal, scores, 0.0).astype(bf16))
+
+    def times(c, matrices):
+        rows = beside(c["parts"])
+        return jnp.concatenate([fold(mm(rows[a], matrices[a])) for a in range(2)], axis=1)
+
+    def inside(c, values):
+        first = mm(c["scores"][0], values[0])
+        return jnp.concatenate([first[:DH], first[DH:] + mm(c["scores"][1], values[1])], axis=0)
+
+    def residual(c):
+        c["residual"] = c["q"].astype(f32) - times(c, c["base"]) - inside(c, c["k"])
+
+    def correct():
+        through("step", 1, lambda c: beside(split(c["residual"])))
+        for group in groups:
+            for c in group:
+                c["s"] = c["s"] + c["step"]
+
+    def readout(c):
+        o_ref[c["at"]] = (times(c, c["prior"]) + inside(c, c["v"])).astype(bf16)
+
+    return [begin] + [each(score), each(residual), correct] * REFINE + [each(score), each(readout)]
+
+
+def precond_kernel(ridge_ref, prior_ref, local_ref, base_ref, y_ref):
+    for step in newton_schulz(ridge_ref, prior_ref, local_ref, base_ref, y_ref):
+        step()
+
+
+def first_kernel(
+    core_ref, q_ref, k_ref, v_ref, y_ref, base_ref, prior_ref, local_ref,
+    ridge_ref, later_prior_ref, later_local_ref, o_ref, later_base_ref, later_y_ref,
+):
+    mine = solving(core_ref[0], q_ref, k_ref, v_ref, y_ref, base_ref, prior_ref, local_ref, o_ref)
+    later = newton_schulz(ridge_ref, later_prior_ref, later_local_ref, later_base_ref, later_y_ref)
+    for i in range(max(len(mine), len(later))):
+        for steps in (mine, later):
+            if i < len(steps):
+                steps[i]()
+
+
+def second_kernel(core_ref, q_ref, k_ref, v_ref, y_ref, base_ref, prior_ref, local_ref, done_ref, o_ref):
+    for step in solving(1 - core_ref[0], q_ref, k_ref, v_ref, y_ref, base_ref, prior_ref, local_ref, o_ref):
+        step()
+
+
+WHOLE = pl.BlockSpec(memory_space=pltpu.VMEM)
+
+
+def part_of(shape, at):
+    return pl.BlockSpec(shape, lambda i, c: (at,) + (0,) * (len(shape) - 1))
+
+
+def call(kernel, core, args, in_specs, out_specs, out_shape, name, **options):
     return pl.pallas_call(
-        precond_kernel,
-        grid=(1,),
-        in_specs=[
-            pl.BlockSpec((half, 8, DH), lambda i: (at, 0, 0)),
-            pl.BlockSpec(prior.shape, lambda i: (0, 0, 0)),
-            pl.BlockSpec((half, 1, DH, DH), lambda i: (at, 2, 0, 0)),
-        ],
-        out_specs=[out, out],
-        out_shape=[shape, shape],
+        kernel,
+        grid_spec=pltpu.PrefetchScalarGridSpec(
+            num_scalar_prefetch=1, grid=(1,), in_specs=in_specs, out_specs=out_specs
+        ),
+        out_shape=out_shape,
         compiler_params=pltpu.CompilerParams(vmem_limit_bytes=VMEM),
+        name=name,
+        **options,
+    )(core, *args)
+
+
+def halves(heads):
+    shape = jax.ShapeDtypeStruct((heads // 2, DH, DH), f32)
+    return [shape, shape]
+
+
+def precond_first_kernel(core_ref, *refs):
+    precond_kernel(*refs)
+
+
+def preconditioners(core, ridge, prior, local):
+    heads = local.shape[0]
+    block = (heads // 2,)
+    return call(
+        precond_first_kernel,
+        core,
+        (ridge, prior, local),
+        [part_of(block + ridge.shape[1:], 0), WHOLE, part_of(block + local.shape[1:], 0)],
+        [WHOLE, WHOLE],
+        halves(heads),
+        "preconditioners",
         cost_estimate=pl.CostEstimate(flops=10**9, bytes_accessed=2 * 10**6, transcendentals=0),
-        name="preconditioners",
-    )(ridge, prior, local)
-
-
-def solve_kernel(core_ref, q_ref, k_ref, v_ref, local_ref, *refs):
-    half_refs, o_ref = refs[:6], refs[6]
-    low = pl.program_id(0) < pl.num_programs(0) // 2
-    shape = (CHUNK, CHUNK)
-    causal = lax.broadcasted_iota(jnp.int32, shape, 0) >= lax.broadcasted_iota(jnp.int32, shape, 1)
-    chains = []
-    for a in range(2):
-        columns = slice(a * DH, (a + 1) * DH)
-        y = side(jnp.where(low, half_refs[0][a], half_refs[1][a]))
-        base = jnp.where(low, half_refs[2][a], half_refs[3][a])
-        cross = jnp.where(low, half_refs[4][0, columns], half_refs[5][0, columns])
-        for j in range(k_ref.shape[0] // CHUNK):
-            rows = slice(j * CHUNK, (j + 1) * CHUNK)
-            if j:
-                base, cross = base + local_ref[a, 0], cross + local_ref[a, 1]
-            chains.append(
-                dict(
-                    at=(rows, columns), q=q_ref[rows, columns], k=k_ref[rows, columns],
-                    v=v_ref[rows, columns], y=y, yy=jnp.concatenate([y, y], axis=0),
-                    base=doubled(base), prior=doubled(cross),
-                )
-            )
-    for c in chains:
-        c["s"] = fold(mm(c["q"], c["y"]))
-    for repeat in range(REFINE):
-        for c in chains:
-            c["parts"] = split(c["s"])
-            c["scores"] = jnp.where(causal, mm_nt(c["parts"][0], c["k"]), 0.0).astype(bf16)
-        for c in chains:
-            product = fold(mm(jnp.concatenate(c["parts"], axis=1), c["base"]))
-            c["residual"] = c["q"].astype(f32) - product - mm(c["scores"], c["k"])
-        for c in chains:
-            c["s"] = c["s"] + fold(mm(side(c["residual"]), c["yy"]))
-    for c in chains:
-        parts = split(c["s"])
-        scores = jnp.where(causal, mm_nt(parts[0], c["k"]), 0.0).astype(bf16)
-        total = fold(mm(jnp.concatenate(parts, axis=1), c["prior"])) + mm(scores, c["v"])
-        o_ref[c["at"]] = total.astype(bf16)
-
-
-def solve(core, query, key, value, local, halves):
+    )
+
+
+def first_solve(core, query, key, value, y, base, prior, local, ridge, later):
     rows, width = query.shape
-    steps = width // DH // 2
-    at_low = lambda i: jnp.minimum(i, steps // 2 - 1)
-    at_high = lambda i: jnp.maximum(i - steps // 2, 0)
-    wide = pl.BlockSpec((rows, 2 * DH), lambda i, c: (0, lax.rem(i + c[0] * (steps // 2), steps)))
-    specs = []
-    for at in (at_low, at_high) * 2:
-        specs.append(pl.BlockSpec((2, DH, DH), lambda i, c, at=at: (at(i), 0, 0)))
-    for at in (at_low, at_high):
-        specs.append(pl.BlockSpec((1, 2 * DH, DH), lambda i, c, at=at: (at(i), 0, 0)))
-    return pl.pallas_call(
-        solve_kernel,
-        grid_spec=pltpu.PrefetchScalarGridSpec(
-            num_scalar_prefetch=1,
-            grid=(steps,),
-            in_specs=[wide, wide, wide, pl.BlockSpec((2, 2, DH, DH), lambda i, c: (i, 0, 0, 0))] + specs,
-            out_specs=wide,
-        ),
-        out_shape=jax.ShapeDtypeStruct((rows, width), bf16),
-        compiler_params=pltpu.CompilerParams(vmem_limit_bytes=VMEM),
-        name="solve",
-    )(core, query, key, value, local, *halves)
+    heads = local.shape[0]
+    block = (heads // 2,)
+    return call(
+        first_kernel,
+        core,
+        (query, key, value, y, base, prior, local, ridge, later, local),
+        [WHOLE] * 6
+        + [part_of(block + local.shape[1:], 0), part_of(block + ridge.shape[1:], 1), WHOLE]
+        + [part_of(block + local.shape[1:], 1)],
+        [pl.BlockSpec((rows, width // 2), lambda i, c: (0, c[0])), WHOLE, WHOLE],
+        [jax.ShapeDtypeStruct((rows, width), bf16)] + halves(heads),
+        "first_solve",
+        cost_estimate=pl.CostEstimate(flops=3 * 10**9, bytes_accessed=2 * 10**6, transcendentals=0),
+    )
+
+
+def second_solve(core, query, key, value, y, base, prior, local, done):
+    rows, width = query.shape
+    block = (local.shape[0] // 2,)
+    return call(
+        second_kernel,
+        core,
+        (query, key, value, y, base, prior, local, done),
+        [WHOLE] * 6 + [part_of(block + local.shape[1:], 1), pl.BlockSpec(memory_space=pl.ANY)],
+        pl.BlockSpec((rows, width // 2), lambda i, c: (0, 1 - c[0])),
+        jax.ShapeDtypeStruct((rows, width), bf16),
+        "second_solve",
+        input_output_aliases={8: 0},
+    )
 
 
 def exchange(x):
@@ -303,11 +419,11 @@
     before = exchange(sums_before(pieces)).reshape(keep.shape)
     mine = before + jnp.where(is_second, received, 0.0)
     other = swapped(before + jnp.where(is_first, keep, 0.0))
-    base0, y0 = preconditioners(ridge, 0, mine, local)
-    base1, y1 = preconditioners(ridge, 1, other, local)
-    return solve(
-        core, query_rows, scaled, value_rows, local, (y0, y1, base0, base1, mine, other)
+    base, y = preconditioners(core, ridge, mine, local)
+    done, base1, y1 = first_solve(
+        core, query_rows, scaled, value_rows, y, base, mine, local, ridge, other
     )
+    return second_solve(core, query_rows, scaled, value_rows, y1, base1, other, local, done)
 
 
 def solution(mesh):

time: 66.9 us -> 64.9 us (0.970)
  Pallas kernels: 16.7 us -> 14.7 us
    pallas_call x3, Pallas kernels: 13.4 us -> 11.4 us  [call(): pl.pallas_call(kernel, grid_spec=pltpu.PrefetchScalarGridSpec(num_scalar_...]
where the time goes in v4:
time: 64.9 us; the launch traced here: 64.7 us
  blocking collectives  41.5 us (64%)
  Pallas kernels  14.7 us (23%)
  starting transfers between devices  6.94 us (11%)
  waiting for transfers between devices  1.38 us (2%)
    all_to_all x2, blocking collectives, exchange(): return lax.all_to_all(x, PLANE, 0, 0)  41.5 us
    pallas_call x3, Pallas kernels, call(): pl.pallas_call(kernel, grid_spec=pltpu.PrefetchScalarGridSpec(num_scalar_...  11.4 us
    ppermute x2, starting transfers between devices, swapped(): return lax.ppermute(x, CORE, [(0, 1), (1, 0)])  6.94 us
    pallas_call x1, Pallas kernels, grams(): pl.pallas_call(gram_kernel, grid_spec=pltpu.PrefetchScalarGridSpec(num_sc...  3.23 us
    ppermute x2, waiting for transfers between devices, swapped(): return lax.ppermute(x, CORE, [(0, 1), (1, 0)])  1.38 us
  transfers between devices with their start and end apart: 2, of which 1 were waited for; matrix products, arithmetic and copies ran while one was open for 0% of the time, Pallas kernels for 3%

profile of v4, /device:TPU:1, one launch (start us, length us, event | category | flops | bytes accessed | tf_op | source)
XLA Modules:
  0.0 64.7 jit_solution(5276175610320573515)
XLA Ops:
  0.0 3.2 %grams.1 = (f32[2,400,128]{2,1,0:T(8,128)S(1)}, f32[2,400,128]{2,1,0:T(8,128)S(1)}, f32[8,3,128,128]{3,2,1,0:T(8,128)S(1)}, bf16[512,1024]{1,0:T(8,128)(2,1)S(1)}, f32[8,8,128]{2,1,0:T(8,128)S(1)}) custom-call(s32[1]{0:T(128)} %bitcast.core_ref, f32[8]{0:T(128)} %gain_ref.1, f32[8]{0:T(128)} %reg_ref.1, bf16[512,1024]{1,0:T(8,128)(2,1)} %k_ref.1, ...), custom_call_target="tpu_custom_call" | custom-call | tf_op jit(solution)/shard_map/grams/pallas_call | solution.py:124
  3.2 3.3 %collective-permute-start = (f32[2,400,128]{2,1,0:T(8,128)S(1)}, f32[2,400,128]{2,1,0:T(8,128)S(1)}, u32[]{:S(2)}, u32[]{:S(2)}) collective-permute-start(f32[2,400,128]{2,1,0:T(8,128)S(1)} %get-tuple-element.22), channel_id=1, source_target_pairs={{0,4},{4,0},{1,5},{5,1},{2,6},{6,2},{3,7},{7,3},{8,12},{12,8},{9,1... | collective-permute-start | bytes 1228808 | tf_op jit(solution)/shard_map/ppermute | solution.py:408
  6.5 1.4 %collective-permute-done = f32[2,400,128]{2,1,0:T(8,128)S(1)} collective-permute-done((f32[2,400,128]{2,1,0:T(8,128)S(1)}, f32[2,400,128]{2,1,0:T(8,128)S(1)}, u32[]{:S(2)}, u32[]{:S(2)}) %collective-permute-start) | collective-permute-done | bytes 409632 | tf_op jit(solution)/shard_map/ppermute | solution.py:408
  7.9 0.1 add.9
  8.0 23.5 %all_to_all.10.x_ref = f32[32,1,3200]{2,1,0:T(1,128)S(1)} all-to-all(f32[32,1,3200]{2,1,0:T(1,128)S(1)} %bitcast.7), channel_id=1, replica_groups=mesh['seq_0'=8,'seq_1'=4,'seq_2'=2,'head'=4] {'seq_0','seq_1'}, dimensions={0} | all-to-all | bytes 819200 | tf_op jit(solution)/shard_map/all_to_all | solution.py:404
  31.5 18.0 %all_to_all.11 = f32[32,1,3200]{2,1,0:T(1,128)S(1)} all-to-all(f32[32,1,3200]{2,1,0:T(1,128)S(1)} %sums_before.1), channel_id=1, replica_groups=mesh['seq_0'=8,'seq_1'=4,'seq_2'=2,'head'=4] {'seq_0','seq_1'}, dimensions={0} | all-to-all | bytes 819200 | tf_op jit(solution)/shard_map/all_to_all | solution.py:404
  49.5 0.1 bitcast_add_fusion
  49.6 3.7 %collective-permute-start.1 = (f32[2,400,128]{2,1,0:T(8,128)S(1)}, f32[2,400,128]{2,1,0:T(8,128)S(1)}, u32[]{:S(2)}, u32[]{:S(2)}) collective-permute-start(f32[2,400,128]{2,1,0:T(8,128)S(1)} %get-tuple-element.31), channel_id=1, source_target_pairs={{0,4},{4,0},{1,5},{5,1},{2,6},{6,2},{3,7},{7,3},{8,12},{12,8},{9,1... | collective-permute-start | bytes 1228808 | tf_op jit(solution)/shard_map/ppermute | solution.py:408
  53.2 0.0 copy-start
  53.2 0.0 copy-start.1
  53.2 2.1 %preconditioners.1 = (f32[4,128,128]{2,1,0:T(8,128)S(1)}, f32[4,128,128]{2,1,0:T(8,128)S(1)}) custom-call(s32[1]{0:T(128)} %bitcast.core_ref, f32[8,8,128]{2,1,0:T(8,128)S(1)} %get-tuple-element.20.refs_0_.ridge_ref, f32[2,400,128]{2,1,0:T(8,128)S(1)} %get-tuple-element.32.refs_1_.prior_ref, ...), custom_call_target="tpu_custom_call" | custom-call | flops 1000000000 | bytes 2000000 | tf_op jit(solution)/shard_map/preconditioners/pallas_call | solution.py:334
  55.4 0.0 collective-permute-done.1.later_prior_ref.prior_ref
  55.4 0.0 copy-done
  55.4 0.0 copy-done.1
  55.4 5.2 %first_solve.1 = (bf16[512,1024]{1,0:T(8,128)(2,1)}, f32[4,128,128]{2,1,0:T(8,128)S(1)}, f32[4,128,128]{2,1,0:T(8,128)S(1)}) custom-call(s32[1]{0:T(128)} %bitcast.core_ref, bf16[512,1024]{1,0:T(8,128)(2,1)S(1)} %copy-done.1, bf16[512,1024]{1,0:T(8,128)(2,1)S(1)} %get-tuple-element.19.k_ref, bf16[512,1024]{1,0:T(8,128)(2,1)S(1)} %copy-done, ...), custom_call_target="tpu_custom_call" | custom-call | flops 3000000000 | bytes 2000000 | tf_op jit(solution)/shard_map/first_solve/pallas_call | solution.py:334
  60.6 4.1 %second_solve.1 = bf16[512,1024]{1,0:T(8,128)(2,1)} custom-call(s32[1]{0:T(128)} %bitcast.core_ref, bf16[512,1024]{1,0:T(8,128)(2,1)S(1)} %copy-done.1, bf16[512,1024]{1,0:T(8,128)(2,1)S(1)} %get-tuple-element.19.k_ref, bf16[512,1024]{1,0:T(8,128)(2,1)S(1)} %copy-done, f32[4,128,128]{2,1,0:T(8,128)S(1)} %get-tuple-element.28.y_ref, ...), custom_call_target="tpu_custom_call", output_to_operand_aliasing={{}: (8, {})} | custom-call | tf_op jit(solution)/shard_map/second_solve/pallas_call | solution.py:334
  (1 shorter events, 0.0 us)
Async XLA Ops:
  3.2 4.7 %collective-permute-start = (f32[2,400,128]{2,1,0:T(8,128)S(1)}, f32[2,400,128]{2,1,0:T(8,128)S(1)}, u32[]{:S(2)}, u32[]{:S(2)}) collective-permute-start(f32[2,400,128]{2,1,0:T(8,128)S(1)} %get-tuple-element.22), channel_id=1, source_target_pairs={{0,4},{4,0},{1,5},{5,1},{2,6},{6,2},{3,7},{7,3},{8,12},{12,8},{9,1... | collective-permute-start | bytes 1228808 | tf_op jit(solution)/shard_map/ppermute | solution.py:408
  49.6 5.8 %collective-permute-start.1 = (f32[2,400,128]{2,1,0:T(8,128)S(1)}, f32[2,400,128]{2,1,0:T(8,128)S(1)}, u32[]{:S(2)}, u32[]{:S(2)}) collective-permute-start(f32[2,400,128]{2,1,0:T(8,128)S(1)} %get-tuple-element.31), channel_id=1, source_target_pairs={{0,4},{4,0},{1,5},{5,1},{2,6},{6,2},{3,7},{7,3},{8,12},{12,8},{9,1... | collective-permute-start | bytes 1228808 | tf_op jit(solution)/shard_map/ppermute | solution.py:408
  53.2 2.2 %copy-start = (bf16[512,1024]{1,0:T(8,128)(2,1)S(1)}, bf16[512,1024]{1,0:T(8,128)(2,1)}, u32[]{:S(2)}) copy-start(bf16[512,1024]{1,0:T(8,128)(2,1)} %v_ref.5) | copy-start | bytes 3145732
  53.2 2.2 %copy-start.1 = (bf16[512,1024]{1,0:T(8,128)(2,1)S(1)}, bf16[512,1024]{1,0:T(8,128)(2,1)}, u32[]{:S(2)}) copy-start(bf16[512,1024]{1,0:T(8,128)(2,1)} %q_ref.3) | copy-start | bytes 3145732

commit v5 on v4

--- a/solution.py
+++ b/solution.py
@@ -65,22 +65,17 @@
     return [pltpu.with_memory_space_constraint(x, pltpu.HBM) for x in arrays]
 
 
-def place_of(core_ref, step, heads):
-    return lax.rem(step + core_ref[0] * (heads // 2), heads)
-
-
 def triangles():
     rows = lax.broadcasted_iota(jnp.int32, (DH, DH), 0)
     columns = lax.broadcasted_iota(jnp.int32, (DH, DH), 1)
     return rows <= columns, rows == columns
 
 
-def gram_kernel(core_ref, gain_ref, reg_ref, k_ref, v_ref, keep_ref, send_ref, local_ref, scaled_ref, ridge_ref):
-    step = pl.program_id(0)
-    heads = 2 * pl.num_programs(0)
+def gram_kernel(which, core_ref, gain_ref, reg_ref, k_ref, v_ref, slab_ref, local_ref, scaled_ref, ridge_ref):
+    half = 1 - core_ref[0] if which else core_ref[0]
     both = []
     for a in range(2):
-        h = place_of(core_ref, 2 * step + a, heads)
+        h = 2 * (half * pl.num_programs(0) + pl.program_id(0)) + a
         columns = slice(a * DH, (a + 1) * DH)
         k = scaled_keys(k_ref[:, columns], gain_ref[h])
         scaled_ref[:, columns] = k
@@ -93,57 +88,41 @@
         local_ref[a, 2] = both[a][:, :DH]
     one, two = both[0][:, :DH], both[1][:, :DH]
     above, on = triangles()
-    packed = jnp.where(above, one, two)
+    for a in range(2):
+        slab_ref[0, a * DH : (a + 1) * DH] = both[a][:, DH:]
+    slab_ref[0, 2 * DH : 3 * DH] = jnp.where(above, one, two)
     diagonal = jnp.sum(jnp.where(on, two, 0.0), axis=0, keepdims=True)
-
-    def put(out_ref):
-        for a in range(2):
-            out_ref[0, a * DH : (a + 1) * DH] = both[a][:, DH:]
-        out_ref[0, 2 * DH : 3 * DH] = packed
-        out_ref[0, 3 * DH :] = jnp.broadcast_to(diagonal, (PAIR - 3 * DH, DH))
-
-    @pl.when(step < heads // 4)
-    def _():
-        put(keep_ref)
-
-    @pl.when(step >= heads // 4)
-    def _():
-        put(send_ref)
-
-
-def grams(core, gain, reg, key, value):
+    slab_ref[0, 3 * DH :] = jnp.broadcast_to(diagonal, (PAIR - 3 * DH, DH))
+
+
+def grams(which, core, gain, reg, key, value):
     gain, reg, key, value = in_hbm(gain, reg, key, value)
     rows, width = key.shape
-    heads = width // DH
-    steps = heads // 2
+    steps = width // DH // 4
     smem = pl.BlockSpec(memory_space=pltpu.SMEM)
-    wide = pl.BlockSpec((rows, 2 * DH), lambda i, c: (0, lax.rem(i + c[0] * (steps // 2), steps)))
-    low = pl.BlockSpec((1, PAIR, DH), lambda i, c: (jnp.minimum(i, steps // 2 - 1), 0, 0))
-    high = pl.BlockSpec((1, PAIR, DH), lambda i, c: (jnp.maximum(i - steps // 2, 0), 0, 0))
-    slabs = jax.ShapeDtypeStruct((steps // 2, PAIR, DH), f32)
+    wide = pl.BlockSpec((rows, 2 * DH), lambda i, c: (0, i + steps * (1 - c[0] if which else c[0])))
     return pl.pallas_call(
-        gram_kernel,
+        functools.partial(gram_kernel, which),
         grid_spec=pltpu.PrefetchScalarGridSpec(
             num_scalar_prefetch=1,
             grid=(steps,),
             in_specs=[smem, smem, wide, wide],
             out_specs=[
-                low,
-                high,
+                pl.BlockSpec((1, PAIR, DH), lambda i, c: (i, 0, 0)),
                 pl.BlockSpec((2, 3, DH, DH), lambda i, c: (i, 0, 0, 0)),
-                wide,
+                pl.BlockSpec((rows, 2 * DH), lambda i, c: (0, i)),
                 pl.BlockSpec((2, 8, DH), lambda i, c: (i, 0, 0)),
             ],
         ),
         out_shape=[
-            slabs,
-            slabs,
-            jax.ShapeDtypeStruct((heads, 3, DH, DH), f32),
-            jax.ShapeDtypeStruct((rows, width), bf16),
-            jax.ShapeDtypeStruct((heads, 8, DH), f32),
+            jax.ShapeDtypeStruct((steps, PAIR, DH), f32),
+            jax.ShapeDtypeStruct((2 * steps, 3, DH, DH), f32),
+            jax.ShapeDtypeStruct((rows, width // 2), bf16),
+            jax.ShapeDtypeStruct((2 * steps, 8, DH), f32),
         ],
         compiler_params=pltpu.CompilerParams(vmem_limit_bytes=VMEM),
-        name="grams",
+        cost_estimate=pl.CostEstimate(flops=10**9, bytes_accessed=2 * 10**6, transcendentals=0),
+        name=f"grams_{which}",
     )(core, gain, reg, key, value)
 
 
@@ -221,7 +200,7 @@
     return [jnp.concatenate([high[a], low[a]], axis=1) for a in range(2)]
 
 
-def solving(half, q_ref, k_ref, v_ref, y_ref, base_ref, prior_ref, local_ref, o_ref):
+def solving(half, q_ref, k_ref, v_ref, y_ref, base_ref, prior_ref, local_ref, o_ref, written=None):
     rows_in = q_ref.shape[0]
     width = q_ref.shape[1] // 2
     groups, weights = [], {}
@@ -239,7 +218,7 @@
                 weights[p, a] = y, jnp.concatenate([y, y], axis=0)
             for j in range(rows_in // CHUNK):
                 rows = slice(j * CHUNK, (j + 1) * CHUNK)
-                k, v = k_ref[rows, columns], v_ref[rows, columns]
+                k, v = k_ref[rows, inside], v_ref[rows, columns]
                 base, prior = [], []
                 for a in range(2):
                     h = 2 * p + a
@@ -282,12 +261,12 @@
         rows = beside(c["parts"])
         return jnp.concatenate([fold(mm(rows[a], matrices[a])) for a in range(2)], axis=1)
 
-    def inside(c, values):
+    def causal_sum(c, values):
         first = mm(c["scores"][0], values[0])
         return jnp.concatenate([first[:DH], first[DH:] + mm(c["scores"][1], values[1])], axis=0)
 
     def residual(c):
-        c["residual"] = c["q"].astype(f32) - times(c, c["base"]) - inside(c, c["k"])
+        c["residual"] = c["q"].astype(f32) - times(c, c["base"]) - causal_sum(c, c["k"])
 
     def correct():
         through("step", 1, lambda c: beside(split(c["residual"])))
@@ -296,7 +275,9 @@
                 c["s"] = c["s"] + c["step"]
 
     def readout(c):
-        o_ref[c["at"]] = (times(c, c["prior"]) + inside(c, c["v"])).astype(bf16)
+        o_ref[c["at"]] = (times(c, c["prior"]) + causal_sum(c, c["v"])).astype(bf16)
+        if written is not None:
+            written(c["at"])
 
     return [begin] + [each(score), each(residual), correct] * REFINE + [each(score), each(readout)]
 
@@ -318,86 +299,75 @@
                 steps[i]()
 
 
-def second_kernel(core_ref, q_ref, k_ref, v_ref, y_ref, base_ref, prior_ref, local_ref, done_ref, o_ref):
-    for step in solving(1 - core_ref[0], q_ref, k_ref, v_ref, y_ref, base_ref, prior_ref, local_ref, o_ref):
+def second_kernel(
+    core_ref, q_ref, k_ref, v_ref, y_ref, base_ref, prior_ref, local_ref, done_ref, o_ref, out_ref, sems
+):
+    width = done_ref.shape[1]
+    half = 1 - core_ref[0]
+    copies = []
+
+    def send(source, rows, start, size, number):
+        columns = pl.ds(pl.multiple_of(start, 2 * DH), size)
+        copies.append(pltpu.make_async_copy(source, o_ref.at[rows, columns], sems.at[number]))
+        copies[-1].start()
+
+    def written(at):
+        rows, columns = at
+        size = columns.stop - columns.start
+        send(out_ref.at[rows, columns], rows, half * width + columns.start, size, len(copies))
+
+    send(done_ref, slice(None), core_ref[0] * width, width, 0)
+    for step in solving(half, q_ref, k_ref, v_ref, y_ref, base_ref, prior_ref, local_ref, out_ref, written):
         step()
+    for copy in copies:
+        copy.wait()
 
 
 WHOLE = pl.BlockSpec(memory_space=pltpu.VMEM)
 
 
-def part_of(shape, at):
-    return pl.BlockSpec(shape, lambda i, c: (at,) + (0,) * (len(shape) - 1))
-
-
-def call(kernel, core, args, in_specs, out_specs, out_shape, name, **options):
+def call(kernel, core, args, out_specs, out_shape, name, flops, scratch=()):
     return pl.pallas_call(
         kernel,
         grid_spec=pltpu.PrefetchScalarGridSpec(
-            num_scalar_prefetch=1, grid=(1,), in_specs=in_specs, out_specs=out_specs
+            num_scalar_prefetch=1, grid=(1,), in_specs=[WHOLE] * len(args), out_specs=out_specs,
+            scratch_shapes=scratch,
         ),
         out_shape=out_shape,
         compiler_params=pltpu.CompilerParams(vmem_limit_bytes=VMEM),
+        cost_estimate=pl.CostEstimate(flops=flops, bytes_accessed=2 * 10**6, transcendentals=0),
         name=name,
-        **options,
     )(core, *args)
-
-
-def halves(heads):
-    shape = jax.ShapeDtypeStruct((heads // 2, DH, DH), f32)
-    return [shape, shape]
 
 
 def precond_first_kernel(core_ref, *refs):
     precond_kernel(*refs)
 
 
+def matrices_like(local):
+    return jax.ShapeDtypeStruct((local.shape[0], DH, DH), f32)
+
+
 def preconditioners(core, ridge, prior, local):
-    heads = local.shape[0]
-    block = (heads // 2,)
-    return call(
-        precond_first_kernel,
-        core,
-        (ridge, prior, local),
-        [part_of(block + ridge.shape[1:], 0), WHOLE, part_of(block + local.shape[1:], 0)],
-        [WHOLE, WHOLE],
-        halves(heads),
-        "preconditioners",
-        cost_estimate=pl.CostEstimate(flops=10**9, bytes_accessed=2 * 10**6, transcendentals=0),
-    )
-
-
-def first_solve(core, query, key, value, y, base, prior, local, ridge, later):
-    rows, width = query.shape
-    heads = local.shape[0]
-    block = (heads // 2,)
-    return call(
-        first_kernel,
-        core,
-        (query, key, value, y, base, prior, local, ridge, later, local),
-        [WHOLE] * 6
-        + [part_of(block + local.shape[1:], 0), part_of(block + ridge.shape[1:], 1), WHOLE]
-        + [part_of(block + local.shape[1:], 1)],
-        [pl.BlockSpec((rows, width // 2), lambda i, c: (0, c[0])), WHOLE, WHOLE],
-        [jax.ShapeDtypeStruct((rows, width), bf16)] + halves(heads),
-        "first_solve",
-        cost_estimate=pl.CostEstimate(flops=3 * 10**9, bytes_accessed=2 * 10**6, transcendentals=0),
-    )
+    shape = matrices_like(local)
+    args = (ridge, prior, local)
+    return call(precond_first_kernel, core, args, [WHOLE] * 2, [shape] * 2, "preconditioners", 10**9)
+
+
+def first_solve(core, query, key, value, y, base, prior, local, ridge, later, later_local):
+    shape = matrices_like(local)
+    args = (query, key, value, y, base, prior, local, ridge, later, later_local)
+    out = jax.ShapeDtypeStruct(key.shape, bf16)
+    return call(first_kernel, core, args, [WHOLE] * 3, [out, shape, shape], "first_solve", 3 * 10**9)
 
 
 def second_solve(core, query, key, value, y, base, prior, local, done):
-    rows, width = query.shape
-    block = (local.shape[0] // 2,)
-    return call(
-        second_kernel,
-        core,
-        (query, key, value, y, base, prior, local, done),
-        [WHOLE] * 6 + [part_of(block + local.shape[1:], 1), pl.BlockSpec(memory_space=pl.ANY)],
-        pl.BlockSpec((rows, width // 2), lambda i, c: (0, 1 - c[0])),
-        jax.ShapeDtypeStruct((rows, width), bf16),
-        "second_solve",
-        input_output_aliases={8: 0},
-    )
+    args = (query, key, value, y, base, prior, local, done)
+    out = jax.ShapeDtypeStruct(query.shape, bf16)
+    units = query.shape[0] // CHUNK * (key.shape[1] // (2 * DH))
+    scratch = [pltpu.VMEM(key.shape, bf16), pltpu.SemaphoreType.DMA((units + 1,))]
+    spec = pl.BlockSpec(memory_space=pltpu.HBM)
+    return call(second_kernel, core, args, spec, out, "second_solve", 3 * 10**9, scratch)
 
 
 def exchange(x):
@@ -413,17 +383,18 @@
     core = place.astype(jnp.int32).reshape(1)
     chips = lax.axis_size(PLANE)
     core, is_first, is_second = lax.optimization_barrier((core, place == 0, place == 1))
-    keep, send, local, scaled, ridge = grams(core, key_gain, regularizer, key_rows, value_rows)
+    send, local1, scaled1, ridge1 = grams(1, core, key_gain, regularizer, key_rows, value_rows)
     received = swapped(send)
+    keep, local0, scaled0, ridge0 = grams(0, core, key_gain, regularizer, key_rows, value_rows)
     pieces = exchange((keep + received).reshape(chips, 1, -1))
     before = exchange(sums_before(pieces)).reshape(keep.shape)
     mine = before + jnp.where(is_second, received, 0.0)
     other = swapped(before + jnp.where(is_first, keep, 0.0))
-    base, y = preconditioners(core, ridge, mine, local)
+    base, y = preconditioners(core, ridge0, mine, local0)
     done, base1, y1 = first_solve(
-        core, query_rows, scaled, value_rows, y, base, mine, local, ridge, other
+        core, query_rows, scaled0, value_rows, y, base, mine, local0, ridge1, other, local1
     )
-    return second_solve(core, query_rows, scaled, value_rows, y1, base1, other, local, done)
+    return second_solve(core, query_rows, scaled1, value_rows, y1, base1, other, local1, done)
 
 
 def solution(mesh):

time: 64.9 us -> 63.4 us (0.977)
  waiting for transfers between devices: 1.38 us -> 0.01 us
    ppermute x2, waiting for transfers between devices: 1.38 us -> 0.01 us  [swapped(): return lax.ppermute(x, CORE, [(0, 1), (1, 0)])]
    pallas_call x3, Pallas kernels: 11.4 us -> 10.8 us  [call(): pl.pallas_call(kernel, grid_spec=pltpu.PrefetchScalarGridSpec(num_scalar_...]
    pallas_call x1 -> x2, Pallas kernels: 3.23 us -> 3.43 us  [grams(): pl.pallas_call(functools.partial(gram_kernel, which), grid_spec=pltpu.Pre...]
  transfers between devices with their start and end apart: 2 -> 2, of which waited for: 1 -> 0; matrix products, arithmetic and copies ran while one was open for 0% -> 0% of each run, Pallas kernels for 3% -> 6%
where the time goes in v5:
time: 63.4 us; the launch traced here: 63.2 us
  blocking collectives  41.4 us (65%)
  Pallas kernels  14.3 us (23%)
  starting transfers between devices  7.16 us (11%)
    all_to_all x2, blocking collectives, exchange(): return lax.all_to_all(x, PLANE, 0, 0)  41.4 us
    pallas_call x3, Pallas kernels, call(): pl.pallas_call(kernel, grid_spec=pltpu.PrefetchScalarGridSpec(num_scalar_...  10.8 us
    ppermute x2, starting transfers between devices, swapped(): return lax.ppermute(x, CORE, [(0, 1), (1, 0)])  7.16 us
    pallas_call x2, Pallas kernels, grams(): pl.pallas_call(functools.partial(gram_kernel, which), grid_spec=pltpu.Pre...  3.43 us
  transfers between devices with their start and end apart: 2, of which 0 were waited for; matrix products, arithmetic and copies ran while one was open for 0% of the time, Pallas kernels for 6%

profile of v5, /device:TPU:1, one launch (start us, length us, event | category | flops | bytes accessed | tf_op | source)
XLA Modules:
  0.0 63.2 jit_solution(17512518081491612318)
XLA Ops:
  0.0 1.7 %grams_1.1 = (f32[2,400,128]{2,1,0:T(8,128)S(1)}, f32[4,3,128,128]{3,2,1,0:T(8,128)S(1)}, bf16[512,512]{1,0:T(8,128)(2,1)S(1)}, f32[4,8,128]{2,1,0:T(8,128)S(1)}) custom-call(s32[1]{0:T(128)} %bitcast.core_ref, f32[8]{0:T(128)} %gain_ref.3, f32[8]{0:T(128)} %reg_ref.3, bf16[512,1024]{1,0:T(8,128)(2,1)} %k_ref.3, bf16[512,1024]{1,0:T(8,128)(2,1)} %v_ref.7), custom_call_target="tpu_custom_call" | custom-call | flops 1000000000 | bytes 2000000 | tf_op jit(solution)/shard_map/grams_1/pallas_call | solution.py:104
  1.7 3.3 %collective-permute-start = (f32[2,400,128]{2,1,0:T(8,128)S(1)}, f32[2,400,128]{2,1,0:T(8,128)S(1)}, u32[]{:S(2)}, u32[]{:S(2)}) collective-permute-start(f32[2,400,128]{2,1,0:T(8,128)S(1)} %get-tuple-element.26), channel_id=1, source_target_pairs={{0,4},{4,0},{1,5},{5,1},{2,6},{6,2},{3,7},{7,3},{8,12},{12,8},{9,1... | collective-permute-start | bytes 1228808 | tf_op jit(solution)/shard_map/ppermute | solution.py:378
  5.0 1.7 %grams_0.1 = (f32[2,400,128]{2,1,0:T(8,128)S(1)}, f32[4,3,128,128]{3,2,1,0:T(8,128)S(1)}, bf16[512,512]{1,0:T(8,128)(2,1)S(1)}, f32[4,8,128]{2,1,0:T(8,128)S(1)}) custom-call(s32[1]{0:T(128)} %bitcast.core_ref, f32[8]{0:T(128)} %gain_ref.3, f32[8]{0:T(128)} %reg_ref.3, bf16[512,1024]{1,0:T(8,128)(2,1)} %k_ref.3, bf16[512,1024]{1,0:T(8,128)(2,1)} %v_ref.7), custom_call_target="tpu_custom_call" | custom-call | flops 1000000000 | bytes 2000000 | tf_op jit(solution)/shard_map/grams_0/pallas_call | solution.py:104
  6.7 0.0 collective-permute-done
  6.7 0.1 add.9
  6.8 24.0 %all_to_all.10.x_ref = f32[32,1,3200]{2,1,0:T(1,128)S(1)} all-to-all(f32[32,1,3200]{2,1,0:T(1,128)S(1)} %bitcast.7), channel_id=1, replica_groups=mesh['seq_0'=8,'seq_1'=4,'seq_2'=2,'head'=4] {'seq_0','seq_1'}, dimensions={0} | all-to-all | bytes 819200 | tf_op jit(solution)/shard_map/all_to_all | solution.py:374
  30.8 17.5 %all_to_all.11 = f32[32,1,3200]{2,1,0:T(1,128)S(1)} all-to-all(f32[32,1,3200]{2,1,0:T(1,128)S(1)} %sums_before.1), channel_id=1, replica_groups=mesh['seq_0'=8,'seq_1'=4,'seq_2'=2,'head'=4] {'seq_0','seq_1'}, dimensions={0} | all-to-all | bytes 819200 | tf_op jit(solution)/shard_map/all_to_all | solution.py:374
  48.3 0.1 bitcast_add_fusion
  48.4 3.9 %collective-permute-start.1 = (f32[2,400,128]{2,1,0:T(8,128)S(1)}, f32[2,400,128]{2,1,0:T(8,128)S(1)}, u32[]{:S(2)}, u32[]{:S(2)}) collective-permute-start(f32[2,400,128]{2,1,0:T(8,128)S(1)} %get-tuple-element.37), channel_id=1, source_target_pairs={{0,4},{4,0},{1,5},{5,1},{2,6},{6,2},{3,7},{7,3},{8,12},{12,8},{9,1... | collective-permute-start | bytes 1228808 | tf_op jit(solution)/shard_map/ppermute | solution.py:378
  52.2 0.0 copy-start
  52.2 0.0 copy-start.1
  52.2 2.1 %preconditioners.1 = (f32[4,128,128]{2,1,0:T(8,128)S(1)}, f32[4,128,128]{2,1,0:T(8,128)S(1)}) custom-call(s32[1]{0:T(128)} %bitcast.core_ref, f32[4,8,128]{2,1,0:T(8,128)S(1)} %get-tuple-element.24.refs_0_, f32[2,400,128]{2,1,0:T(8,128)S(1)} %get-tuple-element.38.refs_1_.prior_ref, f32[4,3,128,128]{3,2,1,0:T(8,128)S(1)} %get-tuple-element.28.refs_2_.local_ref), custom_call_target="tpu_custom_call" | custom-call | flops 1000000000 | bytes 2000000 | tf_op jit(solution)/shard_map/preconditioners/pallas_call | solution.py:330
  54.4 0.0 collective-permute-done.1.later_prior_ref.prior_ref
  54.4 0.0 copy-done
  54.4 0.0 copy-done.1
  54.4 4.5 %first_solve.1 = (bf16[512,512]{1,0:T(8,128)(2,1)S(1)}, f32[4,128,128]{2,1,0:T(8,128)S(1)}, f32[4,128,128]{2,1,0:T(8,128)S(1)}) custom-call(s32[1]{0:T(128)} %bitcast.core_ref, bf16[512,1024]{1,0:T(8,128)(2,1)S(1)} %copy-done, bf16[512,512]{1,0:T(8,128)(2,1)S(1)} %get-tuple-element.23.k_ref, bf16[512,1024]{1,0:T(8,128)(2,1)S(1)} %copy-done.1, ...), custom_call_target="tpu_custom_call" | custom-call | flops 3000000000 | bytes 2000000 | tf_op jit(solution)/shard_map/first_solve/pallas_call | solution.py:330
  59.0 4.1 %second_solve.1 = bf16[512,1024]{1,0:T(8,128)(2,1)} custom-call(s32[1]{0:T(128)} %bitcast.core_ref, bf16[512,1024]{1,0:T(8,128)(2,1)S(1)} %copy-done, bf16[512,512]{1,0:T(8,128)(2,1)S(1)} %get-tuple-element.22.k_ref, bf16[512,1024]{1,0:T(8,128)(2,1)S(1)} %copy-done.1, f32[4,128,128]{2,1,0:T(8,128)S(1)} %get-tuple-element.34.y_ref, ...), custom_call_target="tpu_custom_call" | custom-call | flops 3000000000 | bytes 2000000 | tf_op jit(solution)/shard_map/second_solve/pallas_call | solution.py:330
  (1 shorter events, 0.0 us)
Async XLA Ops:
  1.7 5.0 %collective-permute-start = (f32[2,400,128]{2,1,0:T(8,128)S(1)}, f32[2,400,128]{2,1,0:T(8,128)S(1)}, u32[]{:S(2)}, u32[]{:S(2)}) collective-permute-start(f32[2,400,128]{2,1,0:T(8,128)S(1)} %get-tuple-element.26), channel_id=1, source_target_pairs={{0,4},{4,0},{1,5},{5,1},{2,6},{6,2},{3,7},{7,3},{8,12},{12,8},{9,1... | collective-permute-start | bytes 1228808 | tf_op jit(solution)/shard_map/ppermute | solution.py:378
  48.4 6.0 %collective-permute-start.1 = (f32[2,400,128]{2,1,0:T(8,128)S(1)}, f32[2,400,128]{2,1,0:T(8,128)S(1)}, u32[]{:S(2)}, u32[]{:S(2)}) collective-permute-start(f32[2,400,128]{2,1,0:T(8,128)S(1)} %get-tuple-element.37), channel_id=1, source_target_pairs={{0,4},{4,0},{1,5},{5,1},{2,6},{6,2},{3,7},{7,3},{8,12},{12,8},{9,1... | collective-permute-start | bytes 1228808 | tf_op jit(solution)/shard_map/ppermute | solution.py:378
  52.2 2.2 %copy-start = (bf16[512,1024]{1,0:T(8,128)(2,1)S(1)}, bf16[512,1024]{1,0:T(8,128)(2,1)}, u32[]{:S(2)}) copy-start(bf16[512,1024]{1,0:T(8,128)(2,1)} %q_ref.3) | copy-start | bytes 3145732
  52.2 2.2 %copy-start.1 = (bf16[512,1024]{1,0:T(8,128)(2,1)S(1)}, bf16[512,1024]{1,0:T(8,128)(2,1)}, u32[]{:S(2)}) copy-start(bf16[512,1024]{1,0:T(8,128)(2,1)} %v_ref.7) | copy-start | bytes 3145732

commit v6 on v5

--- a/solution.py
+++ b/solution.py
@@ -14,7 +14,7 @@
 VMEM = 20 * 2**20
 PAIR = 400
 SEQ = ("seq_0", "seq_1", "seq_2")
-PLANE = ("seq_0", "seq_1")
+PLANE = ("seq_1", "seq_0")
 CORE = "seq_2"
 
 f32 = jnp.float32
@@ -126,18 +126,20 @@
     )(core, gain, reg, key, value)
 
 
-def running_kernel(x_ref, o_ref):
+def running_kernel(row, x_ref, o_ref):
+    line = x_ref.shape[0] // row
+    order = [y * line + z for z in range(line) for y in range(row)]
     total = x_ref[0]
     o_ref[0] = jnp.zeros_like(total)
-    for j in range(1, x_ref.shape[0]):
+    for j in order[1:]:
         o_ref[j] = total
-        if j < x_ref.shape[0] - 1:
+        if j != order[-1]:
             total = total + x_ref[j]
 
 
 def sums_before(pieces):
     return pl.pallas_call(
-        running_kernel,
+        functools.partial(running_kernel, lax.axis_size(PLANE[0])),
         out_shape=jax.ShapeDtypeStruct(pieces.shape, f32),
         in_specs=[pl.BlockSpec(memory_space=pltpu.VMEM)],
         out_specs=pl.BlockSpec(memory_space=pltpu.VMEM),
@@ -172,9 +174,10 @@
 
     def step():
         for i in heads:
-            both = jnp.concatenate([approx[i], product[i]], axis=0)
-            both = 2.0 * both - fold(mm(side(both), doubled(product[i])))
-            approx[i], product[i] = both[:DH], both[DH:]
+            rows = side(product[i])
+            weights = jnp.concatenate([rows, rows], axis=0)
+            both = fold(mm(jnp.concatenate([rows, side(approx[i])], axis=0), weights))
+            product[i], approx[i] = 2.0 * product[i] - both[:DH], 2.0 * approx[i] - both[DH:]
 
     def end():
         for i in heads:

time: 63.4 us -> 62.5 us (0.986)
  no operation moved by 1% of the time
where the time goes in v6:
time: 62.5 us; the launch traced here: 62.3 us
  blocking collectives  40.9 us (65%)
  Pallas kernels  14 us (22%)
  starting transfers between devices  7.19 us (12%)
    all_to_all x2, blocking collectives, exchange(): return lax.all_to_all(x, PLANE, 0, 0)  40.9 us
    pallas_call x3, Pallas kernels, call(): pl.pallas_call(kernel, grid_spec=pltpu.PrefetchScalarGridSpec(num_scalar_...  10.6 us
    ppermute x2, starting transfers between devices, swapped(): return lax.ppermute(x, CORE, [(0, 1), (1, 0)])  7.19 us
    pallas_call x2, Pallas kernels, grams(): pl.pallas_call(functools.partial(gram_kernel, which), grid_spec=pltpu.Pre...  3.43 us
  transfers between devices with their start and end apart: 2, of which 0 were waited for; matrix products, arithmetic and copies ran while one was open for 0% of the time, Pallas kernels for 6%

profile of v6, /device:TPU:1, one launch (start us, length us, event | category | flops | bytes accessed | tf_op | source)
XLA Modules:
  0.0 62.3 jit_solution(17087336294179263370)
XLA Ops:
  0.0 1.7 %grams_1.1 = (f32[2,400,128]{2,1,0:T(8,128)S(1)}, f32[4,3,128,128]{3,2,1,0:T(8,128)S(1)}, bf16[512,512]{1,0:T(8,128)(2,1)S(1)}, f32[4,8,128]{2,1,0:T(8,128)S(1)}) custom-call(s32[1]{0:T(128)} %bitcast.core_ref, f32[8]{0:T(128)} %gain_ref.3, f32[8]{0:T(128)} %reg_ref.3, bf16[512,1024]{1,0:T(8,128)(2,1)} %k_ref.3, bf16[512,1024]{1,0:T(8,128)(2,1)} %v_ref.7), custom_call_target="tpu_custom_call" | custom-call | flops 1000000000 | bytes 2000000 | tf_op jit(solution)/shard_map/grams_1/pallas_call | solution.py:104
  1.7 3.3 %collective-permute-start = (f32[2,400,128]{2,1,0:T(8,128)S(1)}, f32[2,400,128]{2,1,0:T(8,128)S(1)}, u32[]{:S(2)}, u32[]{:S(2)}) collective-permute-start(f32[2,400,128]{2,1,0:T(8,128)S(1)} %get-tuple-element.26), channel_id=1, source_target_pairs={{0,4},{4,0},{1,5},{5,1},{2,6},{6,2},{3,7},{7,3},{8,12},{12,8},{9,1... | collective-permute-start | bytes 1228808 | tf_op jit(solution)/shard_map/ppermute | solution.py:381
  5.0 1.7 %grams_0.1 = (f32[2,400,128]{2,1,0:T(8,128)S(1)}, f32[4,3,128,128]{3,2,1,0:T(8,128)S(1)}, bf16[512,512]{1,0:T(8,128)(2,1)S(1)}, f32[4,8,128]{2,1,0:T(8,128)S(1)}) custom-call(s32[1]{0:T(128)} %bitcast.core_ref, f32[8]{0:T(128)} %gain_ref.3, f32[8]{0:T(128)} %reg_ref.3, bf16[512,1024]{1,0:T(8,128)(2,1)} %k_ref.3, bf16[512,1024]{1,0:T(8,128)(2,1)} %v_ref.7), custom_call_target="tpu_custom_call" | custom-call | flops 1000000000 | bytes 2000000 | tf_op jit(solution)/shard_map/grams_0/pallas_call | solution.py:104
  6.7 0.0 collective-permute-done
  6.7 0.1 add.9
  6.8 21.7 %all_to_all.10.x_ref = f32[32,1,3200]{2,1,0:T(1,128)S(1)} all-to-all(f32[32,1,3200]{2,1,0:T(1,128)S(1)} %bitcast.7), channel_id=1, replica_groups=mesh['seq_0'=8,'seq_1'=4,'seq_2'=2,'head'=4] {'seq_1','seq_0'}, dimensions={0} | all-to-all | bytes 819200 | tf_op jit(solution)/shard_map/all_to_all | solution.py:377
  28.5 19.2 %all_to_all.11 = f32[32,1,3200]{2,1,0:T(1,128)S(1)} all-to-all(f32[32,1,3200]{2,1,0:T(1,128)S(1)} %sums_before.1), channel_id=1, replica_groups=mesh['seq_0'=8,'seq_1'=4,'seq_2'=2,'head'=4] {'seq_1','seq_0'}, dimensions={0} | all-to-all | bytes 819200 | tf_op jit(solution)/shard_map/all_to_all | solution.py:377
  47.7 0.1 bitcast_add_fusion
  47.8 3.9 %collective-permute-start.1 = (f32[2,400,128]{2,1,0:T(8,128)S(1)}, f32[2,400,128]{2,1,0:T(8,128)S(1)}, u32[]{:S(2)}, u32[]{:S(2)}) collective-permute-start(f32[2,400,128]{2,1,0:T(8,128)S(1)} %get-tuple-element.37), channel_id=1, source_target_pairs={{0,4},{4,0},{1,5},{5,1},{2,6},{6,2},{3,7},{7,3},{8,12},{12,8},{9,1... | collective-permute-start | bytes 1228808 | tf_op jit(solution)/shard_map/ppermute | solution.py:381
  51.7 0.0 copy-start
  51.7 0.0 copy-start.1
  51.7 1.9 %preconditioners.1 = (f32[4,128,128]{2,1,0:T(8,128)S(1)}, f32[4,128,128]{2,1,0:T(8,128)S(1)}) custom-call(s32[1]{0:T(128)} %bitcast.core_ref, f32[4,8,128]{2,1,0:T(8,128)S(1)} %get-tuple-element.24.refs_0_, f32[2,400,128]{2,1,0:T(8,128)S(1)} %get-tuple-element.38.refs_1_.prior_ref, f32[4,3,128,128]{3,2,1,0:T(8,128)S(1)} %get-tuple-element.28.refs_2_.local_ref), custom_call_target="tpu_custom_call" | custom-call | flops 1000000000 | bytes 2000000 | tf_op jit(solution)/shard_map/preconditioners/pallas_call | solution.py:333
  53.6 0.0 collective-permute-done.1.later_prior_ref.prior_ref
  53.6 0.0 copy-done
  53.7 0.0 copy-done.1
  53.7 4.5 %first_solve.1 = (bf16[512,512]{1,0:T(8,128)(2,1)S(1)}, f32[4,128,128]{2,1,0:T(8,128)S(1)}, f32[4,128,128]{2,1,0:T(8,128)S(1)}) custom-call(s32[1]{0:T(128)} %bitcast.core_ref, bf16[512,1024]{1,0:T(8,128)(2,1)S(1)} %copy-done, bf16[512,512]{1,0:T(8,128)(2,1)S(1)} %get-tuple-element.23.k_ref, bf16[512,1024]{1,0:T(8,128)(2,1)S(1)} %copy-done.1, ...), custom_call_target="tpu_custom_call" | custom-call | flops 3000000000 | bytes 2000000 | tf_op jit(solution)/shard_map/first_solve/pallas_call | solution.py:333
  58.2 4.1 %second_solve.1 = bf16[512,1024]{1,0:T(8,128)(2,1)} custom-call(s32[1]{0:T(128)} %bitcast.core_ref, bf16[512,1024]{1,0:T(8,128)(2,1)S(1)} %copy-done, bf16[512,512]{1,0:T(8,128)(2,1)S(1)} %get-tuple-element.22.k_ref, bf16[512,1024]{1,0:T(8,128)(2,1)S(1)} %copy-done.1, f32[4,128,128]{2,1,0:T(8,128)S(1)} %get-tuple-element.34.y_ref, ...), custom_call_target="tpu_custom_call" | custom-call | flops 3000000000 | bytes 2000000 | tf_op jit(solution)/shard_map/second_solve/pallas_call | solution.py:333
  (1 shorter events, 0.0 us)
Async XLA Ops:
  1.7 5.0 %collective-permute-start = (f32[2,400,128]{2,1,0:T(8,128)S(1)}, f32[2,400,128]{2,1,0:T(8,128)S(1)}, u32[]{:S(2)}, u32[]{:S(2)}) collective-permute-start(f32[2,400,128]{2,1,0:T(8,128)S(1)} %get-tuple-element.26), channel_id=1, source_target_pairs={{0,4},{4,0},{1,5},{5,1},{2,6},{6,2},{3,7},{7,3},{8,12},{12,8},{9,1... | collective-permute-start | bytes 1228808 | tf_op jit(solution)/shard_map/ppermute | solution.py:381
  47.8 5.8 %collective-permute-start.1 = (f32[2,400,128]{2,1,0:T(8,128)S(1)}, f32[2,400,128]{2,1,0:T(8,128)S(1)}, u32[]{:S(2)}, u32[]{:S(2)}) collective-permute-start(f32[2,400,128]{2,1,0:T(8,128)S(1)} %get-tuple-element.37), channel_id=1, source_target_pairs={{0,4},{4,0},{1,5},{5,1},{2,6},{6,2},{3,7},{7,3},{8,12},{12,8},{9,1... | collective-permute-start | bytes 1228808 | tf_op jit(solution)/shard_map/ppermute | solution.py:381
  51.7 1.9 %copy-start = (bf16[512,1024]{1,0:T(8,128)(2,1)S(1)}, bf16[512,1024]{1,0:T(8,128)(2,1)}, u32[]{:S(2)}) copy-start(bf16[512,1024]{1,0:T(8,128)(2,1)} %q_ref.3) | copy-start | bytes 3145732
  51.7 2.0 %copy-start.1 = (bf16[512,1024]{1,0:T(8,128)(2,1)S(1)}, bf16[512,1024]{1,0:T(8,128)(2,1)}, u32[]{:S(2)}) copy-start(bf16[512,1024]{1,0:T(8,128)(2,1)} %v_ref.7) | copy-start | bytes 3145732

commit v7 on v6

--- a/solution.py
+++ b/solution.py
@@ -296,10 +296,10 @@
 ):
     mine = solving(core_ref[0], q_ref, k_ref, v_ref, y_ref, base_ref, prior_ref, local_ref, o_ref)
     later = newton_schulz(ridge_ref, later_prior_ref, later_local_ref, later_base_ref, later_y_ref)
-    for i in range(max(len(mine), len(later))):
-        for steps in (mine, later):
-            if i < len(steps):
-                steps[i]()
+    for i, step in enumerate(mine):
+        step()
+        if i:
+            later[i - 1]()
 
 
 def second_kernel(

time: 62.5 us -> 62.4 us (level)
  no operation moved by 1% of the time
where the time goes in v7:
time: 62.4 us; the launch traced here: 62.2 us
  blocking collectives  40.9 us (66%)
  Pallas kernels  13.9 us (22%)
  starting transfers between devices  7.19 us (12%)
    all_to_all x2, blocking collectives, exchange(): return lax.all_to_all(x, PLANE, 0, 0)  40.9 us
    pallas_call x3, Pallas kernels, call(): pl.pallas_call(kernel, grid_spec=pltpu.PrefetchScalarGridSpec(num_scalar_...  10.5 us
    ppermute x2, starting transfers between devices, swapped(): return lax.ppermute(x, CORE, [(0, 1), (1, 0)])  7.19 us
    pallas_call x2, Pallas kernels, grams(): pl.pallas_call(functools.partial(gram_kernel, which), grid_spec=pltpu.Pre...  3.43 us
  transfers between devices with their start and end apart: 2, of which 0 were waited for; matrix products, arithmetic and copies ran while one was open for 0% of the time, Pallas kernels for 6%

profile of v7, /device:TPU:1, one launch (start us, length us, event | category | flops | bytes accessed | tf_op | source)
XLA Modules:
  0.0 62.2 jit_solution(7267973914255636909)
XLA Ops:
  0.0 1.7 %grams_1.1 = (f32[2,400,128]{2,1,0:T(8,128)S(1)}, f32[4,3,128,128]{3,2,1,0:T(8,128)S(1)}, bf16[512,512]{1,0:T(8,128)(2,1)S(1)}, f32[4,8,128]{2,1,0:T(8,128)S(1)}) custom-call(s32[1]{0:T(128)} %bitcast.core_ref, f32[8]{0:T(128)} %gain_ref.3, f32[8]{0:T(128)} %reg_ref.3, bf16[512,1024]{1,0:T(8,128)(2,1)} %k_ref.3, bf16[512,1024]{1,0:T(8,128)(2,1)} %v_ref.7), custom_call_target="tpu_custom_call" | custom-call | flops 1000000000 | bytes 2000000 | tf_op jit(solution)/shard_map/grams_1/pallas_call | solution.py:104
  1.7 3.3 %collective-permute-start = (f32[2,400,128]{2,1,0:T(8,128)S(1)}, f32[2,400,128]{2,1,0:T(8,128)S(1)}, u32[]{:S(2)}, u32[]{:S(2)}) collective-permute-start(f32[2,400,128]{2,1,0:T(8,128)S(1)} %get-tuple-element.26), channel_id=1, source_target_pairs={{0,4},{4,0},{1,5},{5,1},{2,6},{6,2},{3,7},{7,3},{8,12},{12,8},{9,1... | collective-permute-start | bytes 1228808 | tf_op jit(solution)/shard_map/ppermute | solution.py:381
  5.0 1.7 %grams_0.1 = (f32[2,400,128]{2,1,0:T(8,128)S(1)}, f32[4,3,128,128]{3,2,1,0:T(8,128)S(1)}, bf16[512,512]{1,0:T(8,128)(2,1)S(1)}, f32[4,8,128]{2,1,0:T(8,128)S(1)}) custom-call(s32[1]{0:T(128)} %bitcast.core_ref, f32[8]{0:T(128)} %gain_ref.3, f32[8]{0:T(128)} %reg_ref.3, bf16[512,1024]{1,0:T(8,128)(2,1)} %k_ref.3, bf16[512,1024]{1,0:T(8,128)(2,1)} %v_ref.7), custom_call_target="tpu_custom_call" | custom-call | flops 1000000000 | bytes 2000000 | tf_op jit(solution)/shard_map/grams_0/pallas_call | solution.py:104
  6.7 0.0 collective-permute-done
  6.7 0.1 add.9
  6.8 21.7 %all_to_all.10.x_ref = f32[32,1,3200]{2,1,0:T(1,128)S(1)} all-to-all(f32[32,1,3200]{2,1,0:T(1,128)S(1)} %bitcast.7), channel_id=1, replica_groups=mesh['seq_0'=8,'seq_1'=4,'seq_2'=2,'head'=4] {'seq_1','seq_0'}, dimensions={0} | all-to-all | bytes 819200 | tf_op jit(solution)/shard_map/all_to_all | solution.py:377
  28.5 19.2 %all_to_all.11 = f32[32,1,3200]{2,1,0:T(1,128)S(1)} all-to-all(f32[32,1,3200]{2,1,0:T(1,128)S(1)} %sums_before.1), channel_id=1, replica_groups=mesh['seq_0'=8,'seq_1'=4,'seq_2'=2,'head'=4] {'seq_1','seq_0'}, dimensions={0} | all-to-all | bytes 819200 | tf_op jit(solution)/shard_map/all_to_all | solution.py:377
  47.7 0.1 bitcast_add_fusion
  47.8 3.9 %collective-permute-start.1 = (f32[2,400,128]{2,1,0:T(8,128)S(1)}, f32[2,400,128]{2,1,0:T(8,128)S(1)}, u32[]{:S(2)}, u32[]{:S(2)}) collective-permute-start(f32[2,400,128]{2,1,0:T(8,128)S(1)} %get-tuple-element.37), channel_id=1, source_target_pairs={{0,4},{4,0},{1,5},{5,1},{2,6},{6,2},{3,7},{7,3},{8,12},{12,8},{9,1... | collective-permute-start | bytes 1228808 | tf_op jit(solution)/shard_map/ppermute | solution.py:381
  51.7 0.0 copy-start
  51.7 0.0 copy-start.1
  51.7 1.9 %preconditioners.1 = (f32[4,128,128]{2,1,0:T(8,128)S(1)}, f32[4,128,128]{2,1,0:T(8,128)S(1)}) custom-call(s32[1]{0:T(128)} %bitcast.core_ref, f32[4,8,128]{2,1,0:T(8,128)S(1)} %get-tuple-element.24.refs_0_, f32[2,400,128]{2,1,0:T(8,128)S(1)} %get-tuple-element.38.refs_1_.prior_ref, f32[4,3,128,128]{3,2,1,0:T(8,128)S(1)} %get-tuple-element.28.refs_2_.local_ref), custom_call_target="tpu_custom_call" | custom-call | flops 1000000000 | bytes 2000000 | tf_op jit(solution)/shard_map/preconditioners/pallas_call | solution.py:333
  53.6 0.0 collective-permute-done.1.later_prior_ref.prior_ref
  53.6 0.0 copy-done
  53.7 0.0 copy-done.1
  53.7 4.4 %first_solve.1 = (bf16[512,512]{1,0:T(8,128)(2,1)S(1)}, f32[4,128,128]{2,1,0:T(8,128)S(1)}, f32[4,128,128]{2,1,0:T(8,128)S(1)}) custom-call(s32[1]{0:T(128)} %bitcast.core_ref, bf16[512,1024]{1,0:T(8,128)(2,1)S(1)} %copy-done, bf16[512,512]{1,0:T(8,128)(2,1)S(1)} %get-tuple-element.23.k_ref, bf16[512,1024]{1,0:T(8,128)(2,1)S(1)} %copy-done.1, ...), custom_call_target="tpu_custom_call" | custom-call | flops 3000000000 | bytes 2000000 | tf_op jit(solution)/shard_map/first_solve/pallas_call | solution.py:333
  58.1 4.1 %second_solve.1 = bf16[512,1024]{1,0:T(8,128)(2,1)} custom-call(s32[1]{0:T(128)} %bitcast.core_ref, bf16[512,1024]{1,0:T(8,128)(2,1)S(1)} %copy-done, bf16[512,512]{1,0:T(8,128)(2,1)S(1)} %get-tuple-element.22.k_ref, bf16[512,1024]{1,0:T(8,128)(2,1)S(1)} %copy-done.1, f32[4,128,128]{2,1,0:T(8,128)S(1)} %get-tuple-element.34.y_ref, ...), custom_call_target="tpu_custom_call" | custom-call | flops 3000000000 | bytes 2000000 | tf_op jit(solution)/shard_map/second_solve/pallas_call | solution.py:333
  (1 shorter events, 0.0 us)
Async XLA Ops:
  1.7 5.0 %collective-permute-start = (f32[2,400,128]{2,1,0:T(8,128)S(1)}, f32[2,400,128]{2,1,0:T(8,128)S(1)}, u32[]{:S(2)}, u32[]{:S(2)}) collective-permute-start(f32[2,400,128]{2,1,0:T(8,128)S(1)} %get-tuple-element.26), channel_id=1, source_target_pairs={{0,4},{4,0},{1,5},{5,1},{2,6},{6,2},{3,7},{7,3},{8,12},{12,8},{9,1... | collective-permute-start | bytes 1228808 | tf_op jit(solution)/shard_map/ppermute | solution.py:381
  47.8 5.8 %collective-permute-start.1 = (f32[2,400,128]{2,1,0:T(8,128)S(1)}, f32[2,400,128]{2,1,0:T(8,128)S(1)}, u32[]{:S(2)}, u32[]{:S(2)}) collective-permute-start(f32[2,400,128]{2,1,0:T(8,128)S(1)} %get-tuple-element.37), channel_id=1, source_target_pairs={{0,4},{4,0},{1,5},{5,1},{2,6},{6,2},{3,7},{7,3},{8,12},{12,8},{9,1... | collective-permute-start | bytes 1228808 | tf_op jit(solution)/shard_map/ppermute | solution.py:381
  51.7 1.9 %copy-start = (bf16[512,1024]{1,0:T(8,128)(2,1)S(1)}, bf16[512,1024]{1,0:T(8,128)(2,1)}, u32[]{:S(2)}) copy-start(bf16[512,1024]{1,0:T(8,128)(2,1)} %q_ref.3) | copy-start | bytes 3145732
  51.7 2.0 %copy-start.1 = (bf16[512,1024]{1,0:T(8,128)(2,1)S(1)}, bf16[512,1024]{1,0:T(8,128)(2,1)}, u32[]{:S(2)}) copy-start(bf16[512,1024]{1,0:T(8,128)(2,1)} %v_ref.7) | copy-start | bytes 3145732
